TPU v7x, 256 devices: a whole 4x4x8 slice. The times are simulated.
256 devices in a mesh: row: 8 (over y, z_lo), col: 4 (over z_hi), depth: 8 (over x, core).
Axes of the slice: x: 4, y: 4, z: 8 (z_hi: 4, z_lo: 2; z = z_hi * 2 + z_lo), core: 2. Of those that a mesh axis runs over, the one named last changes fastest.
Arguments:
- grad_out: bfloat16 [2048, 6144], P('depth', 'col'), may hold values from -6 to 6
- pre_act: bfloat16 [2048, 24576], P('depth', 'row'), may hold values from -8 to 8
- down_weight: bfloat16 [24576, 6144], P(('row', 'depth'), 'col'), may hold values from -0.109375 to 0.109375
Outputs:
- grad_pre: bfloat16 [2048, 24576], P('depth', 'row')
- grad_weight: bfloat16 [24576, 6144], P(('row', 'depth'), 'col')
All inputs are finite; a program needn't handle non-finite values.
Results may differ from a plain program's by a relative error of at most 0.0066.
Values may be sent and summed in bfloat16 or wider, within the bound.
A program may use at most 64 MiB of HBM per device.

v0:
```python
import jax
import jax.numpy as jnp
from jax import lax
from jax.sharding import PartitionSpec as P

sqrt_two_pi = 0.7978845608028654
cubic_coeff = 0.044715


def split_up(array, dim, count):
    dims = array.shape
    pieces = array.reshape(*dims[:dim], count, dims[dim] // count, *dims[dim + 1 :])
    return jnp.moveaxis(pieces, dim, 0)


def sum_at_owner(array, axis, dim):
    count = lax.axis_size(axis)
    pieces = lax.all_to_all(split_up(array, dim, count), axis, 0, 0, tiled=True)
    return jnp.sum(pieces.astype(jnp.float32), axis=0)


def sent_to_all(array, axis):
    count = lax.axis_size(axis)
    return lax.all_to_all(
        jnp.broadcast_to(array[None], (count, *array.shape)), axis, 0, 0, tiled=True
    )


def laid_out(pieces, dim):
    dims = list(pieces.shape[1:])
    dims[dim] *= pieces.shape[0]
    return jnp.moveaxis(pieces, 0, dim).reshape(dims)


def collect(array, axis, dim):
    pieces = sent_to_all(array, axis)
    return laid_out(pieces, dim)


def gelu_value(preact):
    tangent = jnp.tanh(sqrt_two_pi * (preact + cubic_coeff * preact * preact * preact))
    return 0.5 * preact * (1.0 + tangent)


def gelu_slope(preact):
    tangent = jnp.tanh(sqrt_two_pi * (preact + cubic_coeff * preact * preact * preact))
    inner = sqrt_two_pi * (1.0 + 3.0 * cubic_coeff * preact * preact)
    return 0.5 * (1.0 + tangent) + 0.5 * preact * (1.0 - tangent * tangent) * inner


def contract_last(left, right):
    return lax.dot_general(
        left, right, (((1,), (1,)), ((), ())), preferred_element_type=jnp.float32
    )


def contract_first(left, right):
    return lax.dot_general(
        left, right, (((0,), (0,)), ((), ())), preferred_element_type=jnp.float32
    )


def finish_rows(partial_value, preacts):
    share = sum_at_owner(partial_value.astype(jnp.bfloat16), "col", 0)
    height = share.shape[0]
    offset = lax.axis_index("col") * height
    pre_rows = lax.dynamic_slice_in_dim(preacts, offset, height, 0)
    pieces = (share * gelu_slope(pre_rows.astype(jnp.float32))).astype(jnp.bfloat16)
    return collect(pieces, "col", 0)


def on_device(grad_out, pre_act, down_weight):
    every_grad = lax.all_gather(grad_out, "depth", axis=0, tiled=True)
    own_pre = lax.all_to_all(pre_act, "depth", split_axis=1, concat_axis=0, tiled=True)
    partial_value = contract_last(every_grad, down_weight)
    local_grad = finish_rows(partial_value, own_pre)
    grad_pre = lax.all_to_all(local_grad, "depth", split_axis=0, concat_axis=1, tiled=True)
    own_act = gelu_value(own_pre.astype(jnp.float32)).astype(jnp.bfloat16)
    grad_weight = contract_first(own_act, every_grad).astype(jnp.bfloat16)
    return (grad_pre, grad_weight)


def solution(mesh):
    placed = (P("depth", "col"), P("depth", "row"), P(("row", "depth"), "col"))
    return jax.shard_map(
        on_device,
        mesh=mesh,
        in_specs=placed,
        out_specs=(P("depth", "row"), P(("row", "depth"), "col")),
        check_vma=False,
    )
```

profile of v0, /device:TPU:56, one launch (start us, length us, event | category | flops | bytes accessed | tf_op | source)
XLA Modules:
  0.0 198.6 jit_solution(504990352886837358)
XLA Ops:
  7.2 0.0 copy-start
  7.2 0.0 all-gather.2.cloned.1.call-start
  7.2 0.7 all-gather.2.cloned.1.call-update
  7.9 2.6 %copy.5 = bf16[256,3072]{0,1:T(8,128)(2,1)} copy(bf16[256,3072]{1,0:T(8,128)(2,1)} %param.4) | data formatting | bytes 3145728 | tf_op args[1]
  10.5 4.3 %all-to-all-start.1 = ((bf16[256,8,384]{0,2,1:T(8,128)(2,1)}), bf16[256,8,384]{0,2,1:T(8,128)(2,1)S(1)}, u32[]{:S(2)}, u32[]{:S(2)}) async-start(bf16[256,8,384]{0,2,1:T(8,128)(2,1)} %bitcast.12), calls=%async_computation.1 | async-start | bytes 3145728 | tf_op jit(solution)/shard_map/all_to_all | solution.py:74
  14.8 48.3 %all-gather.2.cloned.1.call-done = bf16[2048,1536]{1,0:T(8,128)(2,1)} async-done(((bf16[256,1536]{1,0:T(8,128)(2,1)}), bf16[2048,1536]{1,0:T(8,128)(2,1)}) %all-gather.2.cloned.1.call-update) | async-done | bytes 6291472 | tf_op jit(solution)/shard_map/all_gather | solution.py:73
  63.0 0.0 copy-done
  63.0 7.4 %convolution_convert_fusion.1 = bf16[2048,384]{1,0:T(8,128)(2,1)} fusion(bf16[2048,1536]{1,0:T(8,128)(2,1)} %all-gather.2.cloned.1.call-done, bf16[384,1536]{1,0:T(8,128)(2,1)S(1)} %copy-done), kind=kOutput, calls=%fused_computation.12 | convolution fusion | flops 2416705536 | bytes 9043968 | tf_op jit(solution)/shard_map/dot_general | solution.py:52
  70.4 0.0 all-to-all-done.1
  70.4 7.6 %all-to-all-start = ((bf16[4,512,384]{2,1,0:T(8,128)(2,1)}), bf16[4,512,384]{2,1,0:T(8,128)(2,1)}, u32[]{:S(2)}, u32[]{:S(2)}) async-start(bf16[4,512,384]{2,1,0:T(8,128)(2,1)} %bitcast.17), calls=%async_computation | async-start | bytes 3145728 | tf_op jit(solution)/shard_map/all_to_all | solution.py:18
  78.0 1.6 copy.6
  79.5 38.5 %all-to-all-done = bf16[4,512,384]{2,1,0:T(8,128)(2,1)} async-done(((bf16[4,512,384]{2,1,0:T(8,128)(2,1)}), bf16[4,512,384]{2,1,0:T(8,128)(2,1)}, u32[]{:S(2)}, u32[]{:S(2)}) %all-to-all-start) | async-done | bytes 1572896 | tf_op jit(solution)/shard_map/all_to_all | solution.py:18
  118.0 1.7 convert_reduce_fusion
  119.8 1.5 fusion.16
  121.3 0.1 broadcast_in_dim.2
  121.4 41.0 %all_to_all.48 = bf16[4,512,384]{2,1,0:T(8,128)(2,1)} all-to-all(bf16[4,512,384]{2,1,0:T(8,128)(2,1)S(1)} %broadcast_in_dim.2), channel_id=1, replica_groups=mesh['row'=8,'col'=4,'depth'=8] {'col'}, dimensions={0} | all-to-all | bytes 3145728 | tf_op jit(solution)/shard_map/all_to_all | solution.py:24
  162.5 3.6 %all-to-all-start.3 = ((bf16[8,256,384]{2,1,0:T(8,128)(2,1)}), bf16[8,256,384]{2,1,0:T(8,128)(2,1)S(1)}, u32[]{:S(2)}, u32[]{:S(2)}) async-start(bf16[8,256,384]{2,1,0:T(8,128)(2,1)} %bitcast.13), calls=%async_computation.3 | async-start | bytes 3145728 | tf_op jit(solution)/shard_map/all_to_all | solution.py:77
  166.1 7.0 %convolution_convert_fusion = bf16[384,1536]{1,0:T(8,128)(2,1)} fusion(bf16[2048,1536]{1,0:T(8,128)(2,1)} %all-gather.2.cloned.1.call-done, bf16[2048,384]{1,0:T(8,128)(2,1)} %bitcast.16), kind=kOutput, calls=%fused_computation.11 | convolution fusion | flops 2424373248 | bytes 9043968 | tf_op jit(solution)/shard_map/dot_general | solution.py:58
  173.0 14.5 %all-to-all-done.3 = bf16[8,256,384]{2,1,0:T(8,128)(2,1)S(1)} async-done(((bf16[8,256,384]{2,1,0:T(8,128)(2,1)}), bf16[8,256,384]{2,1,0:T(8,128)(2,1)S(1)}, u32[]{:S(2)}, u32[]{:S(2)}) %all-to-all-start.3) | async-done | bytes 1572896 | tf_op jit(solution)/shard_map/all_to_all | solution.py:77
  187.5 1.6 copy.7
  189.2 2.6 %copy.8 = bf16[256,3072]{1,0:T(8,128)(2,1)} copy(bf16[256,3072]{0,1:T(8,128)(2,1)} %bitcast.14) | data formatting | bytes 3145728
Async XLA Ops:
  7.2 55.9 %copy-start = (bf16[384,1536]{1,0:T(8,128)(2,1)S(1)}, bf16[384,1536]{1,0:T(8,128)(2,1)}, u32[]{:S(2)}) copy-start(bf16[384,1536]{1,0:T(8,128)(2,1)} %param.5) | copy-start | bytes 3538948
  7.2 55.9 %all-gather.2.cloned.1.call-start = ((), (), s32[]{:S(2)}) async-start(), calls=%async_computation.4 | async-start | bytes 7077888 | tf_op jit(solution)/shard_map/all_gather | solution.py:73
  10.5 59.9 %all-to-all-start.1 = ((bf16[256,8,384]{0,2,1:T(8,128)(2,1)}), bf16[256,8,384]{0,2,1:T(8,128)(2,1)S(1)}, u32[]{:S(2)}, u32[]{:S(2)}) async-start(bf16[256,8,384]{0,2,1:T(8,128)(2,1)} %bitcast.12), calls=%async_computation.1 | async-start | bytes 3145728 | tf_op jit(solution)/shard_map/all_to_all | solution.py:74
  70.4 47.6 %all-to-all-start = ((bf16[4,512,384]{2,1,0:T(8,128)(2,1)}), bf16[4,512,384]{2,1,0:T(8,128)(2,1)}, u32[]{:S(2)}, u32[]{:S(2)}) async-start(bf16[4,512,384]{2,1,0:T(8,128)(2,1)} %bitcast.17), calls=%async_computation | async-start | bytes 3145728 | tf_op jit(solution)/shard_map/all_to_all | solution.py:18
  162.5 25.1 %all-to-all-start.3 = ((bf16[8,256,384]{2,1,0:T(8,128)(2,1)}), bf16[8,256,384]{2,1,0:T(8,128)(2,1)S(1)}, u32[]{:S(2)}, u32[]{:S(2)}) async-start(bf16[8,256,384]{2,1,0:T(8,128)(2,1)} %bitcast.13), calls=%async_computation.3 | async-start | bytes 3145728 | tf_op jit(solution)/shard_map/all_to_all | solution.py:77
Sparse Core Ops, SparseCore 0:
  9.8 53.1 all-gather.1
where the time goes:
time: 199 us
  waiting for transfers between devices  102 us (51%)
  blocking collectives  41 us (21%)
  starting transfers between devices  15.5 us (8%)
  matrix products  14.4 us (7%)
  between operations  14.1 us (7%)
  local copies, waits for them, and re-layouts  8.49 us (4%)
  other arithmetic  3.26 us (2%)
    all_gather x1, waiting for transfers between devices, on_device(): every_grad = lax.all_gather(grad_out, 'depth', axis=0, tiled=True)  48.3 us
    all_to_all x1, blocking collectives, sent_to_all(): lax.all_to_all(jnp.broadcast_to(array[None], (count, *array.shape)), axis...  41 us
    all_to_all x1, waiting for transfers between devices, sum_at_owner(): pieces = lax.all_to_all(split_up(array, dim, count), axis, 0, 0, tiled=True)  38.5 us
    all_to_all x1, waiting for transfers between devices, on_device(): lax.all_to_all(local_grad, 'depth', split_axis=0, concat_axis=1, tiled=True)  14.5 us
    all_to_all x1, starting transfers between devices, sum_at_owner(): pieces = lax.all_to_all(split_up(array, dim, count), axis, 0, 0, tiled=True)  7.55 us
    dot_general x1, matrix products, contract_last(): lax.dot_general(left, right, (((1,), (1,)), ((), ())), preferred_element_...  7.39 us
    dot_general x1, matrix products, contract_first(): lax.dot_general(left, right, (((0,), (0,)), ((), ())), preferred_element_...  6.99 us
    unnamed x4, local copies, waits for them, and re-layouts  5.16 us
  transfers between devices with their start and end apart: 4, of which 3 were waited for; matrix products, arithmetic and copies ran while one was open for 9% of the time, Pallas kernels for 0%

commit v1 on v0

v1 whole, which is shorter than its diff:
```python
import jax
import jax.numpy as jnp
from jax import lax
from jax.experimental import pallas as pl
from jax.experimental.pallas import tpu as pltpu
from jax.sharding import PartitionSpec as P

sqrt_two_pi = 0.7978845608028654
cubic_coeff = 0.044715
MESH = pl.DeviceIdType.MESH
bf16, f32 = jnp.bfloat16, jnp.float32


def gelu_value(preact):
    tangent = jnp.tanh(sqrt_two_pi * (preact + cubic_coeff * preact * preact * preact))
    return 0.5 * preact * (1.0 + tangent)


def gelu_slope(preact):
    tangent = jnp.tanh(sqrt_two_pi * (preact + cubic_coeff * preact * preact * preact))
    inner = sqrt_two_pi * (1.0 + 3.0 * cubic_coeff * preact * preact)
    return 0.5 * (1.0 + tangent) + 0.5 * preact * (1.0 - tangent * tangent) * inner


def kernel(
    g_hbm, p_hbm, w_hbm, go_hbm, gw_hbm,
    gbuf, pbuf, wbuf, csend, crecv, keep_a, keep_b, keep_own, dsend, ebuf, act_t, gw_buf,
    load_sem, a_recv, p_recv, c_recv, d_recv, e_recv, out_sem,
    a_send, r_send, rx_send, p_send, c_send, d_send, e_send, f_send,
):
    row, col, dep = lax.axis_index("row"), lax.axis_index("col"), lax.axis_index("depth")
    x, core = dep // 2, dep % 2
    other = 1 - core
    chunk = g_hbm.shape[1]
    wide = wbuf.shape[0]
    right, left, far = (x + 1) % 4, (x + 3) % 4, (x + 2) % 4
    up, down = (col + 1) % 4, (col + 3) % 4
    order = [(col + 2) % 4, up, down, col]
    source = {0: x, 1: right, 2: far, 3: left}
    pending = []

    def at_depth(d):
        return (row, col, d)

    def at_col(c):
        return (row, c, dep)

    def send(src, dst, send_sem, recv_sem, device):
        copy = pltpu.make_async_remote_copy(
            src_ref=src, dst_ref=dst, send_sem=send_sem, recv_sem=recv_sem, device_id=device, device_id_type=MESH
        )
        copy.start()
        pending.append(copy)

    def arrived(dst, recv_sem):
        pltpu.make_async_copy(dst, dst, recv_sem).wait()

    loads = {}
    for i, q in enumerate(order):
        loads["g", i] = pltpu.make_async_copy(g_hbm.at[q], gbuf.at[x, q, core], load_sem.at[0, i])
        loads["g", i].start()
    loads["w"] = pltpu.make_async_copy(w_hbm, wbuf, load_sem.at[2, 0])
    loads["w"].start()

    def hidden(d):
        return pl.ds(pl.multiple_of(d * wide, 128), wide)

    for i, q in enumerate(order):
        loads["p", i] = pltpu.make_async_copy(p_hbm.at[q, :, hidden(dep)], pbuf.at[x, q, core], load_sem.at[1, i])
        loads["p", i].start()

    barrier = pltpu.get_barrier_semaphore()
    for t in range(1, 8):
        pl.semaphore_signal(barrier, inc=1, device_id=at_depth((dep + t) % 8), device_id_type=MESH)
    for c in (up, down):
        pl.semaphore_signal(barrier, inc=1, device_id=at_col(c), device_id_type=MESH)
    pl.semaphore_wait(barrier, 9)

    def send_pre(i):
        q = order[i]
        for t in range(1, 8):
            d = (dep + t) % 8
            send(p_hbm.at[q, :, hidden(d)], pbuf.at[x, q, core], p_send.at[i, t], p_recv.at[x, q, core], at_depth(d))

    for i, q in enumerate(order):
        loads["g", i].wait()
        mine = gbuf.at[x, q, core]
        for t, d in enumerate((2 * x + other, 2 * right + core, 2 * left + core)):
            send(mine, mine, a_send.at[i, t], a_recv.at[x, q, core], at_depth(d))
        if i == 2:
            send_pre(3)

    def relay(r, i, onward):
        part = gbuf.at[source[r], order[i], core]
        sem = a_recv.at[source[r], order[i], core]
        arrived(part, sem)
        send(part, part, r_send.at[r, i], sem, at_depth(2 * x + other))
        if onward is not None:
            send(part, part, rx_send.at[i], sem, at_depth(2 * onward + core))

    def partner_part(r, i):
        arrived(gbuf.at[source[r], order[i], other], a_recv.at[source[r], order[i], other])

    def to_col(r, kind, way):
        send(
            csend.at[r, kind, way], crecv.at[r, kind, way], c_send.at[r, kind, way], c_recv.at[r, kind, way],
            at_col((up, down)[way]),
        )

    def group(r, i):
        rows = gbuf[source[r], order[i]].reshape(2 * chunk, gbuf.shape[4])
        part = lax.dot_general(rows, wbuf[...], (((1,), (1,)), ((), ())), preferred_element_type=f32)
        low, high = part[:chunk], part[chunk:]
        if i == 0:
            csend[r, 0, 0] = low.astype(bf16)
            csend[r, 0, 1] = high.astype(bf16)
            to_col(r, 0, 0)
            to_col(r, 0, 1)
        elif i == 1:
            csend[r, 1, 0] = high.astype(bf16)
            keep_a[r] = low
            to_col(r, 1, 0)
        elif i == 2:
            csend[r, 1, 1] = low.astype(bf16)
            keep_b[r] = high
            to_col(r, 1, 1)
        else:
            keep_own[r, 0] = low
            keep_own[r, 1] = high

    def combine(r, way):
        arrived(crecv.at[r, 0, way], c_recv.at[r, 0, way])
        kept = (keep_a, keep_b)[way][r]
        csend[r, 2, way] = (kept + crecv[r, 0, way].astype(f32)).astype(bf16)
        to_col(r, 2, way)

    def finish(r):
        for kind in (1, 2):
            for way in (0, 1):
                arrived(crecv.at[r, kind, way], c_recv.at[r, kind, way])
        s = source[r]
        if r == 0:
            loads["p", 3].wait()
            arrived(pbuf.at[s, col, other], p_recv.at[s, col, other])
        else:
            for k in (0, 1):
                arrived(pbuf.at[s, col, k], p_recv.at[s, col, k])
        for k in (0, 1):
            total = keep_own[r, k] + crecv[r, 2, k].astype(f32) + crecv[r, 1, 1 - k].astype(f32)
            dsend[r, k] = (total * gelu_slope(pbuf[s, col, k].astype(f32))).astype(bf16)
        if r == 0:
            ebuf[col, dep] = dsend[0, core]
            send(
                dsend.at[0, other], ebuf.at[col, dep], d_send.at[0, 0], d_recv.at[dep], at_depth(2 * x + other)
            )
        else:
            for k in (0, 1):
                send(dsend.at[r, k], ebuf.at[col, dep], d_send.at[r, k], d_recv.at[dep], at_depth(2 * s + k))

    outs = []

    def write_out(c, j):
        copy = pltpu.make_async_copy(ebuf.at[c, j], go_hbm.at[c, :, hidden(j)], out_sem.at[c, j])
        copy.start()
        outs.append(copy)

    def e_own(r):
        s = source[r]
        if r == 0:
            arrived(ebuf.at[col, 2 * x + other], d_recv.at[2 * x + other])
        else:
            for k in (0, 1):
                arrived(ebuf.at[col, 2 * s + k], d_recv.at[2 * s + k])
        for k in (0, 1):
            j = 2 * s + k
            for way, c in enumerate((up, down)):
                send(ebuf.at[col, j], ebuf.at[col, j], e_send.at[r, k, way], e_recv.at[way, j], at_col(c))
            write_out(col, j)

    def e_forward(r):
        s = source[r]
        for k, (frm, to) in enumerate(((down, up), (up, down))):
            j = 2 * s + k
            arrived(ebuf.at[frm, j], e_recv.at[k, j])
            send(ebuf.at[frm, j], ebuf.at[frm, j], f_send.at[r, k], e_recv.at[2, j], at_col(to))
            write_out(frm, j)

    def e_rest(r):
        s = source[r]
        for k, frm in enumerate((up, down)):
            j = 2 * s + k
            arrived(ebuf.at[frm, j], e_recv.at[1 - k, j])
            write_out(frm, j)
        for k in (0, 1):
            j = 2 * s + k
            arrived(ebuf.at[(col + 2) % 4, j], e_recv.at[2, j])
            write_out((col + 2) % 4, j)

    def activate(r, i, wait):
        s, q = source[r], order[i]
        if wait:
            if r == 0:
                loads["p", i].wait()
                arrived(pbuf.at[s, q, other], p_recv.at[s, q, other])
            else:
                for k in (0, 1):
                    arrived(pbuf.at[s, q, k], p_recv.at[s, q, k])
        pre = pbuf[s, q].reshape(2 * chunk, wide).astype(f32)
        place = pl.ds(pl.multiple_of((4 * s + q) * 2 * chunk, 128), 2 * chunk)
        act_t[:, place] = gelu_value(pre).astype(bf16).T

    loads["w"].wait()
    for i in range(4):
        partner_part(0, i)
        group(0, i)
    combine(0, 0)
    combine(0, 1)

    for i in range(4):
        relay(3, i, right if i < 2 else None)
        relay(1, i, left if i >= 2 else None)
        for r in (3, 1):
            partner_part(r, i)
            group(r, i)
        if i == 1:
            combine(1, 0)
            combine(3, 0)
            finish(0)
        if i == 2:
            combine(1, 1)
            combine(3, 1)
            e_own(0)
    for i in (0, 2):
        relay(2, i, None)
        partner_part(2, i)
        group(2, i)
    finish(1)
    finish(3)
    send_pre(0)
    for i in (1, 3):
        relay(2, i, None)
        partner_part(2, i)
        group(2, i)
    e_forward(0)
    combine(2, 0)
    combine(2, 1)
    e_own(1)
    e_own(3)
    for r in range(4):
        if r != 2:
            activate(r, 3, False)
    finish(2)
    send_pre(1)
    send_pre(2)
    activate(2, 3, False)
    e_forward(1)
    e_forward(3)
    e_own(2)
    for i in (0, 1, 2):
        for r in range(4):
            activate(r, i, True)
        if i == 1:
            e_forward(2)
            e_rest(0)
    every_grad = gbuf.reshape(gbuf.shape[0] * 8 * chunk, gbuf.shape[4])
    tile = 256
    for n in range(gbuf.shape[4] // tile):
        cols = pl.ds(n * tile, tile)
        gw_buf[:, cols] = jnp.dot(act_t[...], every_grad[:, cols], preferred_element_type=f32).astype(bf16)
        copy = pltpu.make_async_copy(gw_buf.at[:, cols], gw_hbm.at[:, cols], load_sem.at[3, n])
        copy.start()
        outs.append(copy)
        if n == 2:
            e_rest(1)
            e_rest(3)
    e_rest(2)
    for copy in pending:
        copy.wait_send()
    for copy in outs:
        copy.wait()


def on_device(grad_out, pre_act, down_weight):
    tokens, features = grad_out.shape
    hidden = pre_act.shape[1]
    wide = down_weight.shape[0]
    chunk = tokens // 4
    any_spec = pl.BlockSpec(memory_space=pl.ANY)
    dma = pltpu.SemaphoreType.DMA
    grad_pre, grad_weight = pl.pallas_call(
        kernel,
        out_shape=(
            jax.ShapeDtypeStruct((4, chunk, hidden), bf16),
            jax.ShapeDtypeStruct((wide, features), bf16),
        ),
        in_specs=[any_spec] * 3,
        out_specs=(any_spec, any_spec),
        scratch_shapes=[
            pltpu.VMEM((4, 4, 2, chunk, features), bf16),
            pltpu.VMEM((4, 4, 2, chunk, wide), bf16),
            pltpu.VMEM((wide, features), bf16),
            pltpu.VMEM((4, 3, 2, chunk, wide), bf16),
            pltpu.VMEM((4, 3, 2, chunk, wide), bf16),
            pltpu.VMEM((4, chunk, wide), f32),
            pltpu.VMEM((4, chunk, wide), f32),
            pltpu.VMEM((4, 2, chunk, wide), f32),
            pltpu.VMEM((4, 2, chunk, wide), bf16),
            pltpu.VMEM((4, 8, chunk, wide), bf16),
            pltpu.VMEM((wide, 32 * chunk), bf16),
            pltpu.VMEM((wide, features), bf16),
            dma((4, 8)), dma((4, 4, 2)), dma((4, 4, 2)), dma((4, 3, 2)), dma((8,)), dma((3, 8)), dma((4, 8)),
            dma((4, 3)), dma((4, 4)), dma((4,)), dma((4, 8)), dma((4, 3, 2)), dma((4, 2)), dma((4, 2, 2)), dma((4, 2)),
        ],
        compiler_params=pltpu.CompilerParams(collective_id=0, has_side_effects=True),
    )(
        grad_out.reshape(4, chunk, features),
        pre_act.reshape(4, chunk, hidden),
        down_weight,
    )
    return grad_pre.reshape(tokens, hidden), grad_weight


def solution(mesh):
    placed = (P("depth", "col"), P("depth", "row"), P(("row", "depth"), "col"))
    return jax.shard_map(
        on_device,
        mesh=mesh,
        in_specs=placed,
        out_specs=(P("depth", "row"), P(("row", "depth"), "col")),
        check_vma=False,
    )
```

time: 199 us -> 79.3 us (0.40)
  waiting for transfers between devices: 102 us -> 0 us
  Pallas kernels: 0 us -> 74.5 us
  blocking collectives: 41 us -> 0 us
  starting transfers between devices: 15.5 us -> 0 us
  matrix products: 14.4 us -> 0 us
  between operations: 14.1 us -> 0.65 us
  local copies, waits for them, and re-layouts: 8.49 us -> 3.76 us
  other arithmetic: 3.26 us -> 0 us
    pallas_call x0 -> x1, Pallas kernels: none -> 74.5 us  [on_device(): pl.pallas_call(kernel, out_shape=(jax.ShapeDtypeStruct((4, chunk, hidden)...]
    all_to_all x3 -> x0, waiting for transfers between devices: 53 us -> none  [the longest x1 38.5 us: sum_at_owner(): pieces = lax.all_to_all(split_up(array, dim, count), axis, 0, 0, tiled=True)]
    all_gather x1 -> x0, waiting for transfers between devices: 48.3 us -> none  [on_device(): every_grad = lax.all_gather(grad_out, 'depth', axis=0, tiled=True)]
    all_to_all x1 -> x0, blocking collectives: 41 us -> none  [sent_to_all(): lax.all_to_all(jnp.broadcast_to(array[None], (count, *array.shape)), axis...]
    all_to_all x3 -> x0, starting transfers between devices: 15.4 us -> none  [the longest x1 7.55 us: sum_at_owner(): pieces = lax.all_to_all(split_up(array, dim, count), axis, 0, 0, tiled=True)]
    dot_general x2 -> x0, matrix products: 14.4 us -> none  [the longest x1 7.39 us: contract_last(): lax.dot_general(left, right, (((1,), (1,)), ((), ())), preferred_element_...]
    all_to_all x2 -> x0, local copies, waits for them, and re-layouts: 3.19 us -> none  [the longest x1 1.64 us: on_device(): lax.all_to_all(local_grad, 'depth', split_axis=0, concat_axis=1, tiled=True)]
  transfers between devices with their start and end apart: 4 -> 0, of which waited for: 3 -> 0; matrix products, arithmetic and copies ran while one was open for 9% -> 0% of each run, Pallas kernels for 0% -> 0%
where the time goes in v1:
time: 79.3 us; the launch traced here: 78.9 us
  Pallas kernels  74.5 us (94%)
  local copies, waits for them, and re-layouts  3.76 us (5%)
    pallas_call x1, Pallas kernels, on_device(): pl.pallas_call(kernel, out_shape=(jax.ShapeDtypeStruct((4, chunk, hidden)...  74.5 us
    unnamed x4, local copies, waits for them, and re-layouts  3.76 us

profile of v1, /device:TPU:56, one launch (start us, length us, event | category | flops | bytes accessed | tf_op | source)
XLA Modules:
  0.0 78.9 jit_solution(14172686712350660709)
XLA Ops:
  0.6 74.5 %shard_map.50 = (bf16[4,64,3072]{2,1,0:T(8,128)(2,1)}, bf16[384,1536]{1,0:T(8,128)(2,1)}) custom-call(bf16[4,64,1536]{2,1,0:T(8,128)(2,1)} %bitcast.5, bf16[4,64,3072]{2,1,0:T(8,128)(2,1)} %bitcast.3, bf16[384,1536]{1,0:T(8,128)(2,1)} %w_hbm.1), custom_call_target="tpu_custom_call" | custom-call | tf_op jit(solution)/shard_map/pallas_call | solution.py:290
  75.1 0.0 copy-start
  75.1 2.7 %copy.7 = bf16[256,3072]{1,0:T(8,128)(2,1)} copy(bf16[256,3072]{1,0:T(8,128)(2,1)} %bitcast.4) | data formatting | bytes 3145728
  77.9 0.0 copy-done
  77.9 1.0 %copy.8 = bf16[384,1536]{1,0:T(8,128)(2,1)} copy(bf16[384,1536]{1,0:T(8,128)(2,1)S(1)} %copy-done) | data formatting | bytes 2359296
Async XLA Ops:
  75.1 2.8 %copy-start = (bf16[384,1536]{1,0:T(8,128)(2,1)S(1)}, bf16[384,1536]{1,0:T(8,128)(2,1)}, u32[]{:S(2)}) copy-start(bf16[384,1536]{1,0:T(8,128)(2,1)} %get-tuple-element.9) | copy-start | bytes 3538948

commit v2 on v1

v2 whole, which is shorter than its diff:
```python
import jax
import jax.numpy as jnp
from jax import lax
from jax.experimental import pallas as pl
from jax.experimental.pallas import tpu as pltpu
from jax.sharding import PartitionSpec as P

sqrt_two_pi = 0.7978845608028654
cubic_coeff = 0.044715
MESH = pl.DeviceIdType.MESH
bf16, f32 = jnp.bfloat16, jnp.float32


def gelu_value(preact):
    tangent = jnp.tanh(sqrt_two_pi * (preact + cubic_coeff * preact * preact * preact))
    return 0.5 * preact * (1.0 + tangent)


def gelu_slope(preact):
    tangent = jnp.tanh(sqrt_two_pi * (preact + cubic_coeff * preact * preact * preact))
    inner = sqrt_two_pi * (1.0 + 3.0 * cubic_coeff * preact * preact)
    return 0.5 * (1.0 + tangent) + 0.5 * preact * (1.0 - tangent * tangent) * inner


def kernel(
    g_hbm, p_hbm, w_hbm, go, gw,
    gbuf, pbuf, wbuf, first, csend, crecv, keep, keep_own, dsend, act_t, gw_sum,
    load_sem, a_recv, p_recv, c_recv, d_recv, e_recv,
    a_send, r_send, rx_send, p_send, c_send, d_send, e_send, f_send,
):
    row, col, dep = lax.axis_index("row"), lax.axis_index("col"), lax.axis_index("depth")
    x, core = dep // 2, dep % 2
    other = 1 - core
    chunk, features = g_hbm.shape[1:]
    wide = wbuf.shape[0]
    right, left, far = (x + 1) % 4, (x + 3) % 4, (x + 2) % 4
    up, down = (col + 1) % 4, (col + 3) % 4
    order = [(col + 2) % 4, up, down, col]
    source = {0: x, 1: right, 2: far, 3: left}
    pending = []

    def at_depth(d):
        return (row, col, d)

    def at_col(c):
        return (row, c, dep)

    def flush():
        for copy in pending:
            copy.wait_send()
        pending.clear()

    def send(src, dst, send_sem, recv_sem, device):
        copy = pltpu.make_async_remote_copy(
            src_ref=src, dst_ref=dst, send_sem=send_sem, recv_sem=recv_sem, device_id=device, device_id_type=MESH
        )
        copy.start()
        pending.append(copy)

    def arrived(dst, recv_sem):
        pltpu.make_async_copy(dst, dst, recv_sem).wait()

    def hidden(d):
        return pl.ds(pl.multiple_of(d * wide, 128), wide)

    def times_weight(rows):
        return lax.dot_general(rows, wbuf[...], (((1,), (1,)), ((), ())), preferred_element_type=f32)

    barrier = pltpu.get_barrier_semaphore()
    for c in (up, down):
        pl.semaphore_signal(barrier, inc=1, device_id=at_col(c), device_id_type=MESH)
    for t in range(1, 8):
        pl.semaphore_signal(barrier, inc=1, device_id=at_depth((dep + t) % 8), device_id_type=MESH)
    loads = [pltpu.make_async_copy(w_hbm, wbuf, load_sem.at[2, 0])]
    for i, q in enumerate(order):
        loads.append(pltpu.make_async_copy(g_hbm.at[q], gbuf.at[x, q, core], load_sem.at[0, i]))
    for i, q in enumerate(order):
        loads.append(pltpu.make_async_copy(p_hbm.at[q, :, hidden(dep)], pbuf.at[x, q, core], load_sem.at[1, i]))
    for copy in loads:
        copy.start()
    for copy in loads[:5]:
        copy.wait()

    def own_part(k):
        for i, q in enumerate(order):
            first[k, i] = times_weight(gbuf[x, q, k])
        csend[0, 0, k] = first[k, 0].astype(bf16)
        csend[0, 1, 1 - k] = first[k, 2 - k].astype(bf16)
        keep[0, k] = first[k, 1 + k]
        keep_own[0, k] = first[k, 3]

    own_part(core)
    for copy in loads[5:]:
        copy.wait()
    pl.semaphore_wait(barrier, 9)

    def to_col(r, kind, way):
        send(
            csend.at[r, kind, way], crecv.at[r, kind, way], c_send.at[r, kind, way], c_recv.at[r, kind, way],
            at_col((col + 1 + 2 * way) % 4),
        )

    def send_grad(i, devices):
        mine = gbuf.at[x, order[i], core]
        for t, d in devices:
            send(mine, mine, a_send.at[i, t], a_recv.at[x, order[i], core], at_depth(d))

    def send_pre(i, distances):
        q = order[i]
        for t in distances:
            d = (2 * ((x + t) % 4) + core) if t < 4 else (2 * ((x + t - 4) % 4) + other)
            send(p_hbm.at[q, :, hidden(d)], pbuf.at[x, q, core], p_send.at[i, t], p_recv.at[x, q, core], at_depth(d))

    partner = ((0, 2 * x + other),)
    ahead, behind = ((1, 2 * right + core),), ((2, 2 * left + core),)
    send_grad(0, ahead)
    send_grad(0, behind)
    to_col(0, 0, core)
    to_col(0, 1, other)
    for i in range(4):
        send_grad(i, partner)
    for i, j in ((1, 2), (2, 1), (3, 3)):
        send_grad(i, ahead)
        send_grad(j, behind)
    send_pre(3, (1, 3, 5, 7))
    for i in (3, 0, 1, 2):
        send_pre(i, (4,))

    def relay(r, i, onward):
        part = gbuf.at[source[r], order[i], core]
        sem = a_recv.at[source[r], order[i], core]
        arrived(part, sem)
        send(part, part, r_send.at[r, i], sem, at_depth(2 * x + other))
        if onward is not None:
            send(part, part, rx_send.at[i], sem, at_depth(2 * onward + core))

    def partner_part(r, i):
        arrived(gbuf.at[source[r], order[i], other], a_recv.at[source[r], order[i], other])

    def group(r, i):
        part = times_weight(gbuf[source[r], order[i]].reshape(2 * chunk, features))
        low, high = part[:chunk], part[chunk:]
        if i == 0:
            csend[r, 0, 0] = low.astype(bf16)
            csend[r, 0, 1] = high.astype(bf16)
            to_col(r, 0, 0)
            to_col(r, 0, 1)
        elif i == 1:
            csend[r, 1, 0] = high.astype(bf16)
            keep[r, 0] = low
            to_col(r, 1, 0)
        elif i == 2:
            csend[r, 1, 1] = low.astype(bf16)
            keep[r, 1] = high
            to_col(r, 1, 1)
        else:
            keep_own[r, 0] = low
            keep_own[r, 1] = high

    def combine(r, way):
        arrived(crecv.at[r, 0, way], c_recv.at[r, 0, way])
        csend[r, 2, way] = (keep[r, way] + crecv[r, 0, way].astype(f32)).astype(bf16)
        to_col(r, 2, way)

    def pre_arrived(r, i):
        s, q = source[r], order[i]
        if r == 0:
            arrived(pbuf.at[s, q, other], p_recv.at[s, q, other])
        else:
            for k in (0, 1):
                arrived(pbuf.at[s, q, k], p_recv.at[s, q, k])

    def finish(r):
        for kind in (1, 2):
            for way in (0, 1):
                arrived(crecv.at[r, kind, way], c_recv.at[r, kind, way])
        s = source[r]
        for k in (0, 1):
            total = keep_own[r, k] + crecv[r, 2, k].astype(f32) + crecv[r, 1, 1 - k].astype(f32)
            dsend[r, k] = (total * gelu_slope(pbuf[s, col, k].astype(f32))).astype(bf16)
        mine = go.at[col, :, hidden(dep)]
        if r == 0:
            send(dsend.at[0, other], mine, d_send.at[0, 0], d_recv.at[dep], at_depth(2 * x + other))
            go[col, :, hidden(dep)] = dsend[0, core]
        else:
            for k in (0, 1):
                send(dsend.at[r, k], mine, d_send.at[r, k], d_recv.at[dep], at_depth(2 * s + k))

    def piece(c, j):
        return go.at[c, :, hidden(j)]

    def e_own(r):
        s = source[r]
        if r == 0:
            arrived(piece(col, 2 * x + other), d_recv.at[2 * x + other])
        else:
            for k in (0, 1):
                arrived(piece(col, 2 * s + k), d_recv.at[2 * s + k])
        for k in (0, 1):
            j = 2 * s + k
            for way, c in enumerate((up, down)):
                send(piece(col, j), piece(col, j), e_send.at[r, k, way], e_recv.at[way, j], at_col(c))

    def e_forward(r):
        s = source[r]
        for k, (frm, to) in enumerate(((down, up), (up, down))):
            j = 2 * s + k
            arrived(piece(frm, j), e_recv.at[k, j])
            send(piece(frm, j), piece(frm, j), f_send.at[r, k], e_recv.at[2, j], at_col(to))

    def e_rest(r):
        s = source[r]
        for k, frm in enumerate((up, down)):
            j = 2 * s + k
            arrived(piece(frm, j), e_recv.at[1 - k, j])
        for k in (0, 1):
            j = 2 * s + k
            arrived(piece((col + 2) % 4, j), e_recv.at[2, j])

    def activate(r, i):
        s, q = source[r], order[i]
        pre = pbuf[s, q].reshape(2 * chunk, wide).astype(f32)
        place = pl.ds(pl.multiple_of((4 * s + q) * 2 * chunk, 128), 2 * chunk)
        act_t[:, place] = gelu_value(pre).astype(bf16).T

    def weight_grad(r, n):
        s, cols = source[r], pl.ds(n * 512, 512)
        span = 8 * chunk
        part = jnp.dot(
            act_t[:, pl.ds(pl.multiple_of(s * span, 128), span)],
            gbuf[s, :, :, :, cols].reshape(span, 512),
            preferred_element_type=f32,
        )
        if r == 0:
            gw_sum[:, cols] = part
        elif r == 2:
            gw[:, cols] = (gw_sum[:, cols] + part).astype(bf16)
        else:
            gw_sum[:, cols] += part

    def weight_grads(r):
        for n in range(features // 512):
            weight_grad(r, n)

    for i in range(4):
        partner_part(0, i)
    own_part(other)
    to_col(0, 0, other)
    to_col(0, 1, core)
    for i in (3, 0, 1, 2):
        pre_arrived(0, i)
        activate(0, i)
    combine(0, core)
    combine(0, other)

    def two_groups(i, j):
        relay(3, i, right if i < 2 else None)
        relay(1, j, left if j >= 2 else None)
        for r, n in ((3, i), (1, j)):
            partner_part(r, n)
            group(r, n)

    def far_groups(i, j):
        relay(2, i, None)
        relay(2, j, None)
        for n in (i, j):
            partner_part(2, n)
            group(2, n)

    two_groups(0, 0)
    weight_grads(0)
    two_groups(1, 2)
    finish(0)
    two_groups(2, 1)
    e_own(0)
    for way in (0, 1):
        combine(3, way)
        combine(1, 1 - way)
    two_groups(3, 3)
    for r in (1, 3):
        pre_arrived(r, 3)
        activate(r, 3)
    far_groups(0, 2)
    finish(3)
    finish(1)
    send_pre(3, (2, 6))
    send_pre(0, (1, 3, 5, 7))
    e_forward(0)
    far_groups(1, 3)
    combine(2, 0)
    combine(2, 1)
    e_own(1)
    e_own(3)
    pre_arrived(2, 3)
    activate(2, 3)
    finish(2)
    send_pre(1, (1, 3, 5, 7))
    send_pre(2, (1, 3, 5, 7))
    for i in (0, 1, 2):
        send_pre(i, (2, 6))
    e_forward(1)
    e_own(2)
    e_forward(3)
    for i in (0, 1, 2):
        for r in (1, 3):
            pre_arrived(r, i)
            activate(r, i)
    weight_grads(1)
    weight_grads(3)
    e_forward(2)
    e_rest(0)
    for i in (0, 1, 2):
        pre_arrived(2, i)
        activate(2, i)
    weight_grads(2)
    flush()
    e_rest(1)
    e_rest(3)
    e_rest(2)


def on_device(grad_out, pre_act, down_weight):
    tokens, features = grad_out.shape
    hidden = pre_act.shape[1]
    wide = down_weight.shape[0]
    chunk = tokens // 4
    vmem_spec = pl.BlockSpec(memory_space=pltpu.VMEM)
    dma = pltpu.SemaphoreType.DMA
    operands = (grad_out.reshape(4, chunk, features), pre_act.reshape(4, chunk, hidden), down_weight)
    grad_pre, grad_weight = pl.pallas_call(
        kernel,
        out_shape=(
            jax.ShapeDtypeStruct((4, chunk, hidden), bf16),
            jax.ShapeDtypeStruct((wide, features), bf16),
        ),
        in_specs=[pl.BlockSpec(memory_space=pl.ANY)] * 3,
        out_specs=(vmem_spec, vmem_spec),
        scratch_shapes=[
            pltpu.VMEM((4, 4, 2, chunk, features), bf16),
            pltpu.VMEM((4, 4, 2, chunk, wide), bf16),
            pltpu.VMEM((wide, features), bf16),
            pltpu.VMEM((2, 4, chunk, wide), f32),
            pltpu.VMEM((4, 3, 2, chunk, wide), bf16),
            pltpu.VMEM((4, 3, 2, chunk, wide), bf16),
            pltpu.VMEM((4, 2, chunk, wide), f32),
            pltpu.VMEM((4, 2, chunk, wide), f32),
            pltpu.VMEM((4, 2, chunk, wide), bf16),
            pltpu.VMEM((wide, 32 * chunk), bf16),
            pltpu.VMEM((wide, features), f32),
            dma((3, 4)), dma((4, 4, 2)), dma((4, 4, 2)), dma((4, 3, 2)), dma((8,)), dma((3, 8)),
            dma((4, 3)), dma((4, 4)), dma((4,)), dma((4, 8)), dma((4, 3, 2)), dma((4, 2)), dma((4, 2, 2)), dma((4, 2)),
        ],
        compiler_params=pltpu.CompilerParams(
            collective_id=0, has_side_effects=True, vmem_limit_bytes=44 * 1024 * 1024
        ),
    )(*(pltpu.with_memory_space_constraint(operand, pltpu.HBM) for operand in operands))
    return grad_pre.reshape(tokens, hidden), grad_weight


def solution(mesh):
    placed = (P("depth", "col"), P("depth", "row"), P(("row", "depth"), "col"))
    return jax.shard_map(
        on_device,
        mesh=mesh,
        in_specs=placed,
        out_specs=(P("depth", "row"), P(("row", "depth"), "col")),
        check_vma=False,
    )
```

time: 79.3 us -> 73.5 us (0.927); the launches traced: 78.9 us -> 72.2 us
  Pallas kernels: 74.5 us -> 69.4 us
  local copies, waits for them, and re-layouts: 3.76 us -> 2.16 us
    pallas_call x1, Pallas kernels: 74.5 us -> 69.4 us  [on_device(): pl.pallas_call(kernel, out_shape=(jax.ShapeDtypeStruct((4, chunk, hidden)...]
    unnamed x4 -> x2, local copies, waits for them, and re-layouts: 3.76 us -> 2.16 us
where the time goes in v2:
time: 73.5 us; the launch traced here: 72.2 us
  Pallas kernels  69.4 us (94%)
  local copies, waits for them, and re-layouts  2.16 us (3%)
    pallas_call x1, Pallas kernels, on_device(): pl.pallas_call(kernel, out_shape=(jax.ShapeDtypeStruct((4, chunk, hidden)...  69.4 us
    unnamed x2, local copies, waits for them, and re-layouts  2.16 us

profile of v2, /device:TPU:56, one launch (start us, length us, event | category | flops | bytes accessed | tf_op | source)
XLA Modules:
  0.0 72.2 jit_solution(9738054480852043736)
XLA Ops:
  0.6 69.4 %shard_map.50 = (bf16[4,64,3072]{2,1,0:T(8,128)(2,1)S(1)}, bf16[384,1536]{1,0:T(8,128)(2,1)S(1)}) custom-call(bf16[4,64,1536]{2,1,0:T(8,128)(2,1)} %bitcast.5, bf16[4,64,3072]{2,1,0:T(8,128)(2,1)} %bitcast.4, bf16[384,1536]{1,0:T(8,128)(2,1)} %w_hbm.1), custom_call_target="tpu_custom_call" | custom-call | tf_op jit(solution)/shard_map/pallas_call | solution.py:330
  70.0 1.1 %copy.7 = bf16[256,3072]{1,0:T(8,128)(2,1)} copy(bf16[256,3072]{1,0:T(8,128)(2,1)S(1)} %bitcast.3) | data formatting | bytes 3145728
  71.2 1.0 %copy.8 = bf16[384,1536]{1,0:T(8,128)(2,1)} copy(bf16[384,1536]{1,0:T(8,128)(2,1)S(1)} %get-tuple-element.9) | data formatting | bytes 2359296

commit v3 on v0

v3 whole, which is shorter than its diff:
```python
import jax
import jax.numpy as jnp
from jax import lax
from jax.experimental import pallas as pl
from jax.experimental.pallas import tpu as pltpu
from jax.sharding import PartitionSpec as P

sqrt_two_pi = 0.7978845608028654
cubic_coeff = 0.044715
MESH = pl.DeviceIdType.MESH
bf16, f32 = jnp.bfloat16, jnp.float32


def gelu_value(preact):
    tangent = jnp.tanh(sqrt_two_pi * (preact + cubic_coeff * preact * preact * preact))
    return 0.5 * preact * (1.0 + tangent)


def gelu_slope(preact):
    tangent = jnp.tanh(sqrt_two_pi * (preact + cubic_coeff * preact * preact * preact))
    inner = sqrt_two_pi * (1.0 + 3.0 * cubic_coeff * preact * preact)
    return 0.5 * (1.0 + tangent) + 0.5 * preact * (1.0 - tangent * tangent) * inner


PLAN = [
    ("P", 3, 1), ("P", 3, 3), ("A", 0, 3), ("A", 0, 0), ("A", 0, 1), ("A", 0, 2), ("C", 0, 0), ("C", 0, 1), ("X",
    3, 0), ("X", 1, 0), ("G", 3, 0), ("G", 1, 0), ("M", 0, 0), ("M", 0, 1), ("M", 0, 2), ("X", 3, 1), ("X", 1, 2),
    ("G", 3, 1), ("G", 1, 2), ("F", 0), ("X", 3, 2), ("X", 1, 1), ("G", 3, 2), ("G", 1, 1), ("O", 0), ("C", 3, 0),
    ("C", 1, 1), ("C", 3, 1), ("C", 1, 0), ("X", 3, 3), ("X", 1, 3), ("Y", 3, 3), ("Y", 1, 3), ("G", 3, 3), ("G",
    1, 3), ("A", 1, 3), ("A", 3, 3), ("X", 2, 0), ("X", 2, 2), ("G", 2, 0), ("G", 2, 2), ("F", 3), ("F", 1), ("P",
    3, 2), ("P", 0, 1), ("P", 0, 3), ("W", 0), ("X", 2, 1), ("X", 2, 3), ("Y", 2, 3), ("G", 2, 1), ("G", 2, 3),
    ("C", 2, 0), ("C", 2, 1), ("O", 1), ("O", 3), ("A", 2, 3), ("F", 2), ("P", 1, 1), ("P", 1, 3), ("P", 2, 1),
    ("P", 2, 3), ("P", 0, 2), ("P", 1, 2), ("P", 2, 2), ("W", 1), ("O", 2), ("W", 3), ("A", 1, 0), ("A", 1, 1),
    ("A", 1, 2), ("A", 3, 0), ("A", 3, 1), ("A", 3, 2), ("M", 1, 0), ("M", 1, 1), ("M", 1, 2), ("M", 3, 0), ("M",
    3, 1), ("M", 3, 2), ("W", 2), ("R", 0), ("A", 2, 0), ("A", 2, 1), ("A", 2, 2), ("M", 2, 0), ("M", 2, 1), ("M",
    2, 2), ("R", 1), ("R", 3), ("R", 2),
]


WHOLE = (0, 1, 2)

def kernel(
    g_hbm, p_hbm, w_hbm, go, gw,
    gbuf, pbuf, wbuf, first, csend, crecv, keep, keep_own, dsend, act_t, gw_sum, gw_buf,
    load_sem, out_sem, s_recv, a_recv, p_recv, c_recv, d_recv, e_recv, sent,
):
    row, col, dep = lax.axis_index("row"), lax.axis_index("col"), lax.axis_index("depth")
    x, core = dep // 2, dep % 2
    other = 1 - core
    part_rows, features = g_hbm.shape[2:]
    chunk = 2 * part_rows
    wide = wbuf.shape[0]
    y = row // 2
    half = y % 2
    north, south = (row + 2) % 8, (row + 6) % 8
    right, left, far = (x + 1) % 4, (x + 3) % 4, (x + 2) % 4
    up, down = (col + 1) % 4, (col + 3) % 4
    order = [(col + 2) % 4, up, down, col]
    source = {0: x, 1: right, 2: far, 3: left}
    local = []

    def at_depth(d):
        return (row, col, d)

    def at_col(c):
        return (row, c, dep)

    GRAD, PRE, SUM, SHARE, SPREAD = range(5)

    def send(kind, src, dst, recv_sem, device):
        pltpu.make_async_remote_copy(
            src_ref=src, dst_ref=dst, send_sem=sent.at[kind], recv_sem=recv_sem, device_id=device, device_id_type=MESH
        ).start()

    def arrived(dst, recv_sem):
        pltpu.make_async_copy(dst, dst, recv_sem).wait()

    def hidden(d):
        return pl.ds(pl.multiple_of(d * wide, 128), wide)

    def times_weight(rows):
        return lax.dot_general(rows, wbuf[...], (((1,), (1,)), ((), ())), preferred_element_type=f32)

    barrier = pltpu.get_barrier_semaphore()
    for c in (up, down):
        pl.semaphore_signal(barrier, inc=1, device_id=at_col(c), device_id_type=MESH)
    for t in range(1, 8):
        pl.semaphore_signal(barrier, inc=1, device_id=at_depth((dep + t) % 8), device_id_type=MESH)
    for n in (north, south):
        pl.semaphore_signal(barrier, inc=1, device_id=(n, col, dep), device_id_type=MESH)
    loads = [
        pltpu.make_async_copy(w_hbm, wbuf, load_sem.at[0]),
        pltpu.make_async_copy(g_hbm, gbuf.at[x, :, core], load_sem.at[1]),
        pltpu.make_async_copy(p_hbm.at[:, :, hidden(dep)], pbuf.at[x, :, core], load_sem.at[2]),
    ]
    for copy in loads:
        copy.start()
    loads[0].wait()
    loads[1].wait()

    def own_part(k):
        rows = gbuf[x, :, k].reshape(4 * chunk, features)
        first[k] = times_weight(rows).reshape(4, chunk, wide)
        csend[0, 0, k] = first[k, order[0]].astype(bf16)
        csend[0, 1, 1 - k] = first[k, (col + 3 + 2 * k) % 4].astype(bf16)
        keep[0, k] = first[k, (col + 1 + 2 * k) % 4]
        keep_own[0, k] = first[k, col]

    own_part(core)
    loads[2].wait()
    pl.semaphore_wait(barrier, 11)

    def to_col(r, kind, way):
        sem = c_recv.at[r, way] if kind == 0 else c_recv.at[r, 2]
        send(SUM, csend.at[r, kind, way], crecv.at[r, kind, way], sem, at_col((col + 1 + 2 * way) % 4))

    def send_grad(i, r, d):
        mine = gbuf.at[x, order[i], core] if i in WHOLE else gbuf.at[x, order[i], core, half]
        send(GRAD, mine, mine, a_recv.at[r - 1, i, 0], at_depth(d))

    def send_pre(i, t):
        q = order[i]
        sem = p_recv.at[(4 - t) % 4, 0 if i == 3 else 1]
        for d in (2 * ((x + t) % 4) + core, 2 * ((x + t) % 4) + other)[0 if t else 1 :]:
            send(PRE, p_hbm.at[q, :, hidden(d)], pbuf.at[x, q, core], sem, at_depth(d))

    send_grad(0, 3, 2 * right + core)
    send_grad(0, 1, 2 * left + core)
    to_col(0, 0, core)
    to_col(0, 1, other)
    mine = gbuf.at[x, :, core]
    send(GRAD, mine, mine, s_recv, at_depth(2 * x + other))
    for i, j in ((1, 2), (2, 1), (3, 3)):
        send_grad(i, 3, 2 * right + core)
        send_grad(j, 1, 2 * left + core)
    for i in (3, 0, 1, 2):
        send_pre(i, 0)

    def from_x(r, i):
        part, sem = gbuf.at[source[r], order[i], core], a_recv.at[r - 1, i]
        if i not in WHOLE:
            part = part.at[half]
        arrived(part, sem.at[0])
        from_left = r == 3 or (r == 2 and i < 2)
        if i not in WHOLE:
            send(GRAD, part, part, sem.at[1], (north if from_left else south, col, dep))
        send(GRAD, part, part, sem.at[2], at_depth(2 * x + other))
        if r == 3 and i < 2:
            send(GRAD, part, part, a_recv.at[1, i, 0], at_depth(2 * right + core))
        if r == 1 and i >= 2:
            send(GRAD, part, part, a_recv.at[1, i, 0], at_depth(2 * left + core))

    def from_y(r, i):
        if i in WHOLE:
            return
        part, sem = gbuf.at[source[r], order[i], core, 1 - half], a_recv.at[r - 1, i]
        arrived(part, sem.at[1])
        send(GRAD, part, part, sem.at[2], at_depth(2 * x + other))

    def group(r, i):
        s, q = source[r], order[i]
        arrived(gbuf.at[s, q, other], a_recv.at[r - 1, i, 2])
        part = times_weight(gbuf[s, q].reshape(2 * chunk, features))
        low, high = part[:chunk], part[chunk:]
        if i == 0:
            csend[r, 0, 0] = low.astype(bf16)
            csend[r, 0, 1] = high.astype(bf16)
            to_col(r, 0, 0)
            to_col(r, 0, 1)
        elif i == 1:
            csend[r, 1, 0] = high.astype(bf16)
            keep[r, 0] = low
            to_col(r, 1, 0)
        elif i == 2:
            csend[r, 1, 1] = low.astype(bf16)
            keep[r, 1] = high
            to_col(r, 1, 1)
        else:
            keep_own[r, 0] = low
            keep_own[r, 1] = high

    def combine(r, way):
        arrived(crecv.at[r, 0, way], c_recv.at[r, way])
        csend[r, 2, way] = (keep[r, way] + crecv[r, 0, way].astype(f32)).astype(bf16)
        to_col(r, 2, way)

    seen = set()

    def pre_arrived(r, i):
        s, rest = source[r], int(i < 3)
        if (r, rest) not in seen:
            seen.add((r, rest))
            chunks = pl.ds(0, 3 if rest else 1)
            arrived(pbuf.at[s, chunks, 0] if r == 0 else pbuf.at[s, chunks], p_recv.at[r, rest])

    def finish(r):
        arrived(crecv.at[r, pl.ds(1, 2)], c_recv.at[r, 2])
        pre_arrived(r, 3)
        s = source[r]
        for k in (0, 1):
            total = keep_own[r, k] + crecv[r, 2, k].astype(f32) + crecv[r, 1, 1 - k].astype(f32)
            dsend[r, k] = (total * gelu_slope(pbuf[s, col, k].astype(f32))).astype(bf16)
        mine = go.at[col, :, hidden(dep)]
        if r == 0:
            send(SHARE, dsend.at[0, other], mine, d_recv.at[0], at_depth(2 * x + other))
            local.append(pltpu.make_async_copy(dsend.at[0, core], mine, out_sem.at[0]))
            local[-1].start()
        else:
            for k in (0, 1):
                send(SHARE, dsend.at[r, k], mine, d_recv.at[4 - r], at_depth(2 * s + k))

    def piece(c, j):
        return go.at[c, :, hidden(j)]

    def e_own(r):
        s = source[r]
        if r == 0:
            arrived(piece(col, 2 * x + other), d_recv.at[0])
            local.pop(0).wait()
        else:
            arrived(dsend.at[r], d_recv.at[r])
        for flip in (0, 1):
            for k in (0, 1):
                part = piece(col, 2 * s + k)
                send(SPREAD, part, part, e_recv.at[r, 2 if flip else k], at_col((up, down)[k ^ flip]))

    def e_forward(r):
        for k, (frm, to) in enumerate(((down, up), (up, down))):
            part = piece(frm, 2 * source[r] + k)
            arrived(part, e_recv.at[r, k])
            send(SPREAD, part, part, e_recv.at[r, 2], at_col(to))

    def e_rest(r):
        arrived(crecv.at[r, pl.ds(0, 2)], e_recv.at[r, 2])

    def activate(r, i):
        pre_arrived(r, i)
        s, q = source[r], order[i]
        pre = pbuf[s, q].reshape(2 * chunk, wide).astype(f32)
        place = pl.ds(pl.multiple_of((4 * s + q) * 2 * chunk, 128), 2 * chunk)
        act_t[:, place] = gelu_value(pre).astype(bf16).T

    def weight_grad(r, n):
        s, cols = source[r], pl.ds(n * 512, 512)
        span = 8 * chunk
        part = jnp.dot(
            act_t[:, pl.ds(pl.multiple_of(s * span, 128), span)],
            gbuf[s, :, :, :, :, cols].reshape(span, 512),
            preferred_element_type=f32,
        )
        if r == 0:
            gw_sum[:, cols] = part
        elif r == 2:
            gw_buf[:, cols] = (gw_sum[:, cols] + part).astype(bf16)
            local.append(pltpu.make_async_copy(gw_buf.at[:, cols], gw.at[:, cols], out_sem.at[1 + n]))
            local[-1].start()
        else:
            gw_sum[:, cols] += part

    arrived(gbuf.at[x, :, other], s_recv)
    own_part(other)
    to_col(0, 0, other)
    to_col(0, 1, core)

    steps = dict(
        X=from_x, Y=from_y, G=group, C=combine, F=finish, O=e_own, W=e_forward, R=e_rest, A=activate, M=weight_grad,
        P=send_pre,
    )
    for name, *numbers in PLAN:
        steps[name](*numbers)
    every_grad = gbuf.reshape(64, part_rows, features)
    arrived(every_grad.at[pl.ds(0, 56)], sent.at[GRAD])
    arrived(pbuf.reshape(32, chunk, wide).at[pl.ds(0, 28)], sent.at[PRE])
    arrived(crecv, sent.at[SUM])
    arrived(dsend.reshape(8, chunk, wide).at[pl.ds(0, 7)], sent.at[SHARE])
    arrived(crecv, sent.at[SPREAD])
    for copy in local:
        copy.wait()


def write_results(go, gw, go_out, gw_out, sem):
    copies = []
    for n, (src, dst) in enumerate(((go, go_out), (gw, gw_out))):
        rows = src.shape[0] // 4
        for i in range(4):
            part = pl.ds(i * rows, rows)
            copies.append(pltpu.make_async_copy(src.at[part], dst.at[part], sem.at[n, i]))
    for copy in copies:
        copy.start()
    for copy in copies:
        copy.wait()


def on_device(grad_out, pre_act, down_weight):
    tokens, features = grad_out.shape
    hidden = pre_act.shape[1]
    wide = down_weight.shape[0]
    chunk = tokens // 4
    any_spec = pl.BlockSpec(memory_space=pl.ANY)
    dma = pltpu.SemaphoreType.DMA
    operands = (grad_out.reshape(4, 2, chunk // 2, features), pre_act.reshape(4, chunk, hidden), down_weight)
    grad_pre, grad_weight = pl.pallas_call(
        kernel,
        out_shape=(
            jax.ShapeDtypeStruct((4, chunk, hidden), bf16),
            jax.ShapeDtypeStruct((wide, features), bf16),
        ),
        in_specs=[any_spec] * 3,
        out_specs=(any_spec, any_spec),
        scratch_shapes=[
            pltpu.VMEM((4, 4, 2, 2, chunk // 2, features), bf16),
            pltpu.VMEM((4, 4, 2, chunk, wide), bf16),
            pltpu.VMEM((wide, features), bf16),
            pltpu.VMEM((2, 4, chunk, wide), f32),
            pltpu.VMEM((4, 3, 2, chunk, wide), bf16),
            pltpu.VMEM((4, 3, 2, chunk, wide), bf16),
            pltpu.VMEM((4, 2, chunk, wide), f32),
            pltpu.VMEM((4, 2, chunk, wide), f32),
            pltpu.VMEM((4, 2, chunk, wide), bf16),
            pltpu.VMEM((wide, 32 * chunk), bf16),
            pltpu.VMEM((wide, features), f32),
            pltpu.VMEM((wide, features), bf16),
            dma((3,)), dma((4,)), dma(()), dma((3, 4, 3)), dma((4, 2)), dma((4, 3)), dma((4,)), dma((4, 3)), dma((5,)),
        ],
        compiler_params=pltpu.CompilerParams(
            collective_id=0, has_side_effects=True, vmem_limit_bytes=44 * 1024 * 1024
        ),
    )(*(pltpu.with_memory_space_constraint(operand, pltpu.HBM) for operand in operands))
    return pl.pallas_call(
        write_results,
        out_shape=(
            jax.ShapeDtypeStruct((tokens, hidden), bf16),
            jax.ShapeDtypeStruct((wide, features), bf16),
        ),
        in_specs=[any_spec] * 2,
        out_specs=(any_spec, any_spec),
        scratch_shapes=[dma((2, 4))],
        compiler_params=pltpu.CompilerParams(vmem_limit_bytes=1024 * 1024),
    )(grad_pre.reshape(tokens, hidden), grad_weight)


def solution(mesh):
    placed = (P("depth", "col"), P("depth", "row"), P(("row", "depth"), "col"))
    return jax.shard_map(
        on_device,
        mesh=mesh,
        in_specs=placed,
        out_specs=(P("depth", "row"), P(("row", "depth"), "col")),
        check_vma=False,
    )
```

time: 199 us -> 76.8 us (0.39)
  the two profiles are of different devices: /device:TPU:56 before, /device:TPU:54 now
where the time goes in v3:
time: 76.8 us; the launch traced here: 76.7 us
  Pallas kernels  76.1 us (99%)
    pallas_call x1, Pallas kernels, on_device(): pl.pallas_call(kernel, out_shape=(jax.ShapeDtypeStruct((4, chunk, hidden)...  74.5 us
    pallas_call x1, Pallas kernels, on_device(): pl.pallas_call(write_results, out_shape=(jax.ShapeDtypeStruct((tokens, hi...  1.59 us

profile of v3, /device:TPU:54, one launch (start us, length us, event | category | flops | bytes accessed | tf_op | source)
XLA Modules:
  0.0 76.7 jit_solution(1753534612600300570)
XLA Ops:
  0.6 74.5 %shard_map.50 = (bf16[4,64,3072]{2,1,0:T(8,128)(2,1)S(1)}, bf16[384,1536]{1,0:T(8,128)(2,1)S(1)}) custom-call(bf16[4,2,32,1536]{3,2,1,0:T(8,128)(2,1)} %bitcast.5, bf16[4,64,3072]{2,1,0:T(8,128)(2,1)} %bitcast.4, bf16[384,1536]{1,0:T(8,128)(2,1)} %w_hbm.1), custom_call_target="tpu_custom_call" | custom-call | tf_op jit(solution)/shard_map/pallas_call | solution.py:302
  75.1 1.6 %shard_map.51 = (bf16[256,3072]{1,0:T(8,128)(2,1)}, bf16[384,1536]{1,0:T(8,128)(2,1)}) custom-call(bf16[256,3072]{1,0:T(8,128)(2,1)S(1)} %bitcast.3, bf16[384,1536]{1,0:T(8,128)(2,1)S(1)} %get-tuple-element.5.gw), custom_call_target="tpu_custom_call" | custom-call | tf_op jit(solution)/shard_map/pallas_call | solution.py:329

commit v4 on v3

--- a/solution.py
+++ b/solution.py
@@ -23,21 +23,19 @@
 
 
 PLAN = [
-    ("P", 3, 1), ("P", 3, 3), ("A", 0, 3), ("A", 0, 0), ("A", 0, 1), ("A", 0, 2), ("C", 0, 0), ("C", 0, 1), ("X",
-    3, 0), ("X", 1, 0), ("G", 3, 0), ("G", 1, 0), ("M", 0, 0), ("M", 0, 1), ("M", 0, 2), ("X", 3, 1), ("X", 1, 2),
-    ("G", 3, 1), ("G", 1, 2), ("F", 0), ("X", 3, 2), ("X", 1, 1), ("G", 3, 2), ("G", 1, 1), ("O", 0), ("C", 3, 0),
-    ("C", 1, 1), ("C", 3, 1), ("C", 1, 0), ("X", 3, 3), ("X", 1, 3), ("Y", 3, 3), ("Y", 1, 3), ("G", 3, 3), ("G",
-    1, 3), ("A", 1, 3), ("A", 3, 3), ("X", 2, 0), ("X", 2, 2), ("G", 2, 0), ("G", 2, 2), ("F", 3), ("F", 1), ("P",
-    3, 2), ("P", 0, 1), ("P", 0, 3), ("W", 0), ("X", 2, 1), ("X", 2, 3), ("Y", 2, 3), ("G", 2, 1), ("G", 2, 3),
-    ("C", 2, 0), ("C", 2, 1), ("O", 1), ("O", 3), ("A", 2, 3), ("F", 2), ("P", 1, 1), ("P", 1, 3), ("P", 2, 1),
-    ("P", 2, 3), ("P", 0, 2), ("P", 1, 2), ("P", 2, 2), ("W", 1), ("O", 2), ("W", 3), ("A", 1, 0), ("A", 1, 1),
-    ("A", 1, 2), ("A", 3, 0), ("A", 3, 1), ("A", 3, 2), ("M", 1, 0), ("M", 1, 1), ("M", 1, 2), ("M", 3, 0), ("M",
-    3, 1), ("M", 3, 2), ("W", 2), ("R", 0), ("A", 2, 0), ("A", 2, 1), ("A", 2, 2), ("M", 2, 0), ("M", 2, 1), ("M",
-    2, 2), ("R", 1), ("R", 3), ("R", 2),
+    ("P", 3, 3), ("X", 3, 0), ("X", 1, 0), ("C", 0, 0), ("G", 1, 0), ("X", 1, 4), ("X", 3, 4), ("C", 0, 1), ("G",
+    3, 4), ("G", 3, 0), ("X", 3, 1), ("X", 1, 2), ("G", 1, 4), ("A", 0, 3), ("G", 3, 1), ("G", 1, 2), ("A", 0, 0),
+    ("F", 0), ("X", 3, 2), ("O", 0), ("X", 1, 1), ("G", 1, 1), ("X", 3, 3), ("C", 1, 1), ("X", 1, 3), ("G", 3, 2),
+    ("C", 1, 0), ("X", 2, 0), ("G", 1, 3), ("G", 3, 3), ("P", 3, 1), ("X", 2, 4), ("G", 2, 0), ("G", 2, 4), ("C",
+    3, 1), ("C", 3, 0), ("P", 0, 3), ("X", 2, 1), ("W", 0), ("X", 2, 2), ("F", 1), ("P", 3, 2), ("P", 0, 1), ("G",
+    2, 1), ("G", 2, 2), ("X", 2, 3), ("P", 1, 1), ("C", 2, 1), ("A", 0, 1), ("C", 2, 0), ("A", 0, 2), ("F", 3),
+    ("P", 2, 3), ("O", 3), ("P", 1, 3), ("M", 0, 2), ("A", 3, 3), ("G", 2, 3), ("M", 0, 0), ("O", 1), ("F", 2),
+    ("P", 1, 2), ("W", 3), ("P", 2, 1), ("O", 2), ("P", 2, 2), ("P", 0, 2), ("W", 1), ("A", 1, 0), ("R", 0), ("A",
+    1, 2), ("A", 2, 3), ("W", 2), ("A", 1, 3), ("A", 3, 1), ("A", 3, 0), ("A", 3, 2), ("M", 0, 1), ("M", 3, 1),
+    ("A", 2, 1), ("M", 3, 0), ("A", 1, 1), ("M", 3, 2), ("A", 2, 2), ("M", 1, 0), ("A", 2, 0), ("R", 3), ("M", 1,
+    2), ("M", 1, 1), ("M", 2, 1), ("M", 2, 0), ("M", 2, 2), ("R", 1), ("R", 2),
 ]
 
-
-WHOLE = (0, 1, 2)
 
 def kernel(
     g_hbm, p_hbm, w_hbm, go, gw,
@@ -50,9 +48,6 @@
     part_rows, features = g_hbm.shape[2:]
     chunk = 2 * part_rows
     wide = wbuf.shape[0]
-    y = row // 2
-    half = y % 2
-    north, south = (row + 2) % 8, (row + 6) % 8
     right, left, far = (x + 1) % 4, (x + 3) % 4, (x + 2) % 4
     up, down = (col + 1) % 4, (col + 3) % 4
     order = [(col + 2) % 4, up, down, col]
@@ -86,8 +81,6 @@
         pl.semaphore_signal(barrier, inc=1, device_id=at_col(c), device_id_type=MESH)
     for t in range(1, 8):
         pl.semaphore_signal(barrier, inc=1, device_id=at_depth((dep + t) % 8), device_id_type=MESH)
-    for n in (north, south):
-        pl.semaphore_signal(barrier, inc=1, device_id=(n, col, dep), device_id_type=MESH)
     loads = [
         pltpu.make_async_copy(w_hbm, wbuf, load_sem.at[0]),
         pltpu.make_async_copy(g_hbm, gbuf.at[x, :, core], load_sem.at[1]),
@@ -108,14 +101,20 @@
 
     own_part(core)
     loads[2].wait()
-    pl.semaphore_wait(barrier, 11)
-
-    def to_col(r, kind, way):
+    pl.semaphore_wait(barrier, 9)
+
+    def to_col(r, kind, way, rows=slice(None)):
         sem = c_recv.at[r, way] if kind == 0 else c_recv.at[r, 2]
-        send(SUM, csend.at[r, kind, way], crecv.at[r, kind, way], sem, at_col((col + 1 + 2 * way) % 4))
+        src, dst = csend.at[r, kind, way, rows], crecv.at[r, kind, way, rows]
+        send(SUM, src, dst, sem, at_col((col + 1 + 2 * way) % 4))
+
+    def token_rows(s, i, c):
+        if i % 4:
+            return gbuf.at[s, order[i], c]
+        return gbuf.at[s, order[0], c, i // 4]
 
     def send_grad(i, r, d):
-        mine = gbuf.at[x, order[i], core] if i in WHOLE else gbuf.at[x, order[i], core, half]
+        mine = token_rows(x, i, core)
         send(GRAD, mine, mine, a_recv.at[r - 1, i, 0], at_depth(d))
 
     def send_pre(i, t):
@@ -130,44 +129,35 @@
     to_col(0, 1, other)
     mine = gbuf.at[x, :, core]
     send(GRAD, mine, mine, s_recv, at_depth(2 * x + other))
-    for i, j in ((1, 2), (2, 1), (3, 3)):
+    for i, j in ((4, 4), (1, 2), (2, 1), (3, 3)):
         send_grad(i, 3, 2 * right + core)
         send_grad(j, 1, 2 * left + core)
     for i in (3, 0, 1, 2):
         send_pre(i, 0)
 
     def from_x(r, i):
-        part, sem = gbuf.at[source[r], order[i], core], a_recv.at[r - 1, i]
-        if i not in WHOLE:
-            part = part.at[half]
+        part, sem = token_rows(source[r], i, core), a_recv.at[r - 1, i]
         arrived(part, sem.at[0])
-        from_left = r == 3 or (r == 2 and i < 2)
-        if i not in WHOLE:
-            send(GRAD, part, part, sem.at[1], (north if from_left else south, col, dep))
-        send(GRAD, part, part, sem.at[2], at_depth(2 * x + other))
-        if r == 3 and i < 2:
+        send(GRAD, part, part, sem.at[1], at_depth(2 * x + other))
+        if r == 3 and i in (0, 4, 1):
             send(GRAD, part, part, a_recv.at[1, i, 0], at_depth(2 * right + core))
-        if r == 1 and i >= 2:
+        if r == 1 and i in (2, 3):
             send(GRAD, part, part, a_recv.at[1, i, 0], at_depth(2 * left + core))
 
-    def from_y(r, i):
-        if i in WHOLE:
+    def group(r, i):
+        s = source[r]
+        arrived(token_rows(s, i, other), a_recv.at[r - 1, i, 1])
+        if i % 4 == 0:
+            h = i // 4
+            part = times_weight(gbuf[s, order[0], :, h].reshape(chunk, features)).astype(bf16)
+            rows = pl.ds(h * part_rows, part_rows)
+            for way in (0, 1):
+                csend[r, 0, way, rows] = part[way * part_rows : (way + 1) * part_rows]
+                to_col(r, 0, way, rows)
             return
-        part, sem = gbuf.at[source[r], order[i], core, 1 - half], a_recv.at[r - 1, i]
-        arrived(part, sem.at[1])
-        send(GRAD, part, part, sem.at[2], at_depth(2 * x + other))
-
-    def group(r, i):
-        s, q = source[r], order[i]
-        arrived(gbuf.at[s, q, other], a_recv.at[r - 1, i, 2])
-        part = times_weight(gbuf[s, q].reshape(2 * chunk, features))
+        part = times_weight(gbuf[s, order[i]].reshape(2 * chunk, features))
         low, high = part[:chunk], part[chunk:]
-        if i == 0:
-            csend[r, 0, 0] = low.astype(bf16)
-            csend[r, 0, 1] = high.astype(bf16)
-            to_col(r, 0, 0)
-            to_col(r, 0, 1)
-        elif i == 1:
+        if i == 1:
             csend[r, 1, 0] = high.astype(bf16)
             keep[r, 0] = low
             to_col(r, 1, 0)
@@ -180,6 +170,8 @@
             keep_own[r, 1] = high
 
     def combine(r, way):
+        if r == 0:
+            way = (core, other)[way]
         arrived(crecv.at[r, 0, way], c_recv.at[r, way])
         csend[r, 2, way] = (keep[r, way] + crecv[r, 0, way].astype(f32)).astype(bf16)
         to_col(r, 2, way)
@@ -263,7 +255,7 @@
     to_col(0, 1, core)
 
     steps = dict(
-        X=from_x, Y=from_y, G=group, C=combine, F=finish, O=e_own, W=e_forward, R=e_rest, A=activate, M=weight_grad,
+        X=from_x, G=group, C=combine, F=finish, O=e_own, W=e_forward, R=e_rest, A=activate, M=weight_grad,
         P=send_pre,
     )
     for name, *numbers in PLAN:
@@ -320,7 +312,7 @@
             pltpu.VMEM((wide, 32 * chunk), bf16),
             pltpu.VMEM((wide, features), f32),
             pltpu.VMEM((wide, features), bf16),
-            dma((3,)), dma((4,)), dma(()), dma((3, 4, 3)), dma((4, 2)), dma((4, 3)), dma((4,)), dma((4, 3)), dma((5,)),
+            dma((3,)), dma((4,)), dma(()), dma((3, 5, 2)), dma((4, 2)), dma((4, 3)), dma((4,)), dma((4, 3)), dma((5,)),
         ],
         compiler_params=pltpu.CompilerParams(
             collective_id=0, has_side_effects=True, vmem_limit_bytes=44 * 1024 * 1024

time: 76.8 us -> 68.4 us (0.89)
  the two profiles are of different devices: /device:TPU:54 before, /device:TPU:56 now
where the time goes in v4:
time: 68.4 us; the launch traced here: 68.3 us
  Pallas kernels  67.7 us (99%)
    pallas_call x1, Pallas kernels, on_device(): pl.pallas_call(kernel, out_shape=(jax.ShapeDtypeStruct((4, chunk, hidden)...  66.1 us
    pallas_call x1, Pallas kernels, on_device(): pl.pallas_call(write_results, out_shape=(jax.ShapeDtypeStruct((tokens, hi...  1.59 us

profile of v4, /device:TPU:56, one launch (start us, length us, event | category | flops | bytes accessed | tf_op | source)
XLA Modules:
  0.0 68.3 jit_solution(9691527448812124139)
XLA Ops:
  0.6 66.1 %shard_map.50 = (bf16[4,64,3072]{2,1,0:T(8,128)(2,1)S(1)}, bf16[384,1536]{1,0:T(8,128)(2,1)S(1)}) custom-call(bf16[4,2,32,1536]{3,2,1,0:T(8,128)(2,1)} %bitcast.5, bf16[4,64,3072]{2,1,0:T(8,128)(2,1)} %bitcast.4, bf16[384,1536]{1,0:T(8,128)(2,1)} %w_hbm.1), custom_call_target="tpu_custom_call" | custom-call | tf_op jit(solution)/shard_map/pallas_call | solution.py:294
  66.7 1.6 %shard_map.51 = (bf16[256,3072]{1,0:T(8,128)(2,1)}, bf16[384,1536]{1,0:T(8,128)(2,1)}) custom-call(bf16[256,3072]{1,0:T(8,128)(2,1)S(1)} %bitcast.3, bf16[384,1536]{1,0:T(8,128)(2,1)S(1)} %get-tuple-element.5.gw), custom_call_target="tpu_custom_call" | custom-call | tf_op jit(solution)/shard_map/pallas_call | solution.py:321

commit v5 on v4

--- a/solution.py
+++ b/solution.py
@@ -22,18 +22,20 @@
     return 0.5 * (1.0 + tangent) + 0.5 * preact * (1.0 - tangent * tangent) * inner
 
 
+SPLIT = (0,)
+
 PLAN = [
-    ("P", 3, 3), ("X", 3, 0), ("X", 1, 0), ("C", 0, 0), ("G", 1, 0), ("X", 1, 4), ("X", 3, 4), ("C", 0, 1), ("G",
-    3, 4), ("G", 3, 0), ("X", 3, 1), ("X", 1, 2), ("G", 1, 4), ("A", 0, 3), ("G", 3, 1), ("G", 1, 2), ("A", 0, 0),
-    ("F", 0), ("X", 3, 2), ("O", 0), ("X", 1, 1), ("G", 1, 1), ("X", 3, 3), ("C", 1, 1), ("X", 1, 3), ("G", 3, 2),
-    ("C", 1, 0), ("X", 2, 0), ("G", 1, 3), ("G", 3, 3), ("P", 3, 1), ("X", 2, 4), ("G", 2, 0), ("G", 2, 4), ("C",
-    3, 1), ("C", 3, 0), ("P", 0, 3), ("X", 2, 1), ("W", 0), ("X", 2, 2), ("F", 1), ("P", 3, 2), ("P", 0, 1), ("G",
-    2, 1), ("G", 2, 2), ("X", 2, 3), ("P", 1, 1), ("C", 2, 1), ("A", 0, 1), ("C", 2, 0), ("A", 0, 2), ("F", 3),
-    ("P", 2, 3), ("O", 3), ("P", 1, 3), ("M", 0, 2), ("A", 3, 3), ("G", 2, 3), ("M", 0, 0), ("O", 1), ("F", 2),
-    ("P", 1, 2), ("W", 3), ("P", 2, 1), ("O", 2), ("P", 2, 2), ("P", 0, 2), ("W", 1), ("A", 1, 0), ("R", 0), ("A",
-    1, 2), ("A", 2, 3), ("W", 2), ("A", 1, 3), ("A", 3, 1), ("A", 3, 0), ("A", 3, 2), ("M", 0, 1), ("M", 3, 1),
-    ("A", 2, 1), ("M", 3, 0), ("A", 1, 1), ("M", 3, 2), ("A", 2, 2), ("M", 1, 0), ("A", 2, 0), ("R", 3), ("M", 1,
-    2), ("M", 1, 1), ("M", 2, 1), ("M", 2, 0), ("M", 2, 2), ("R", 1), ("R", 2),
+    ("X", 1, 0), ("X", 3, 0), ("G", 3, 0), ("C", 0, 0), ("C", 0, 1), ("A", 0, 3), ("X", 3, 4), ("G", 1, 0), ("X",
+    1, 4), ("G", 3, 4), ("X", 1, 2), ("G", 1, 4), ("X", 3, 1), ("G", 1, 2), ("G", 3, 1), ("F", 0), ("O", 0), ("P",
+    3, 3), ("X", 1, 1), ("G", 1, 1), ("C", 1, 1), ("A", 0, 1), ("X", 3, 2), ("X", 1, 3), ("P", 3, 1), ("G", 3, 2),
+    ("X", 3, 3), ("C", 1, 0), ("P", 0, 3), ("C", 3, 0), ("C", 3, 1), ("A", 0, 2), ("G", 1, 3), ("A", 0, 0), ("X",
+    2, 4), ("X", 2, 0), ("G", 2, 0), ("G", 2, 4), ("X", 2, 2), ("P", 2, 3), ("W", 0), ("X", 2, 1), ("F", 1), ("G",
+    2, 2), ("P", 3, 2), ("M", 0, 1), ("G", 2, 1), ("G", 3, 3), ("F", 3), ("C", 2, 1), ("P", 1, 3), ("P", 2, 1),
+    ("X", 2, 3), ("C", 2, 0), ("P", 1, 1), ("P", 0, 1), ("G", 2, 3), ("O", 3), ("M", 0, 0), ("F", 2), ("O", 1),
+    ("A", 1, 2), ("A", 1, 0), ("W", 3), ("M", 0, 2), ("A", 3, 3), ("A", 1, 1), ("P", 2, 2), ("A", 3, 1), ("O", 2),
+    ("A", 2, 3), ("P", 0, 2), ("A", 3, 0), ("W", 1), ("A", 1, 3), ("P", 1, 2), ("W", 2), ("R", 3), ("M", 1, 1),
+    ("A", 3, 2), ("A", 2, 2), ("M", 3, 0), ("A", 2, 0), ("M", 1, 2), ("M", 1, 0), ("A", 2, 1), ("M", 2, 0), ("M",
+    3, 2), ("M", 2, 2), ("M", 3, 1), ("M", 2, 1), ("R", 2), ("R", 0), ("R", 1),
 ]
 
 
@@ -94,12 +96,15 @@
     def own_part(k):
         rows = gbuf[x, :, k].reshape(4 * chunk, features)
         first[k] = times_weight(rows).reshape(4, chunk, wide)
-        csend[0, 0, k] = first[k, order[0]].astype(bf16)
         csend[0, 1, 1 - k] = first[k, (col + 3 + 2 * k) % 4].astype(bf16)
         keep[0, k] = first[k, (col + 1 + 2 * k) % 4]
         keep_own[0, k] = first[k, col]
 
+    def far_part(k):
+        csend[0, 0, k] = times_weight(gbuf[x, order[0], k].reshape(chunk, features)).astype(bf16)
+
     own_part(core)
+    csend[0, 0, core] = first[core, order[0]].astype(bf16)
     loads[2].wait()
     pl.semaphore_wait(barrier, 9)
 
@@ -109,9 +114,8 @@
         send(SUM, src, dst, sem, at_col((col + 1 + 2 * way) % 4))
 
     def token_rows(s, i, c):
-        if i % 4:
-            return gbuf.at[s, order[i], c]
-        return gbuf.at[s, order[0], c, i // 4]
+        whole = gbuf.at[s, order[i % 4], c]
+        return whole.at[i // 4] if i % 4 in SPLIT else whole
 
     def send_grad(i, r, d):
         mine = token_rows(x, i, core)
@@ -127,11 +131,15 @@
     send_grad(0, 1, 2 * left + core)
     to_col(0, 0, core)
     to_col(0, 1, other)
-    mine = gbuf.at[x, :, core]
-    send(GRAD, mine, mine, s_recv, at_depth(2 * x + other))
-    for i, j in ((4, 4), (1, 2), (2, 1), (3, 3)):
-        send_grad(i, 3, 2 * right + core)
-        send_grad(j, 1, 2 * left + core)
+    for i, q in enumerate(order):
+        mine = gbuf.at[x, q, core]
+        send(GRAD, mine, mine, s_recv.at[min(i, 1)], at_depth(2 * x + other))
+    for i, j in ((0, 0), (1, 2), (2, 1), (3, 3)):
+        for h in (0, 1):
+            if h == 1 and i in SPLIT or h == 0 and i != 0:
+                send_grad(i + 4 * h, 3, 2 * right + core)
+            if h == 1 and j in SPLIT or h == 0 and j != 0:
+                send_grad(j + 4 * h, 1, 2 * left + core)
     for i in (3, 0, 1, 2):
         send_pre(i, 0)
 
@@ -139,35 +147,38 @@
         part, sem = token_rows(source[r], i, core), a_recv.at[r - 1, i]
         arrived(part, sem.at[0])
         send(GRAD, part, part, sem.at[1], at_depth(2 * x + other))
-        if r == 3 and i in (0, 4, 1):
+        if r == 3 and i % 4 < 2:
             send(GRAD, part, part, a_recv.at[1, i, 0], at_depth(2 * right + core))
-        if r == 1 and i in (2, 3):
+        if r == 1 and i % 4 >= 2:
             send(GRAD, part, part, a_recv.at[1, i, 0], at_depth(2 * left + core))
 
     def group(r, i):
         s = source[r]
         arrived(token_rows(s, i, other), a_recv.at[r - 1, i, 1])
-        if i % 4 == 0:
-            h = i // 4
-            part = times_weight(gbuf[s, order[0], :, h].reshape(chunk, features)).astype(bf16)
-            rows = pl.ds(h * part_rows, part_rows)
-            for way in (0, 1):
-                csend[r, 0, way, rows] = part[way * part_rows : (way + 1) * part_rows]
-                to_col(r, 0, way, rows)
-            return
-        part = times_weight(gbuf[s, order[i]].reshape(2 * chunk, features))
-        low, high = part[:chunk], part[chunk:]
-        if i == 1:
-            csend[r, 1, 0] = high.astype(bf16)
-            keep[r, 0] = low
-            to_col(r, 1, 0)
+        q, h, count, i = order[i % 4], i // 4, part_rows, i % 4
+        if i in SPLIT:
+            tokens = gbuf[s, q, :, h]
+        else:
+            tokens, count = gbuf[s, q], chunk
+        part = times_weight(tokens.reshape(2 * count, features))
+        low, high = part[:count], part[count:]
+        rows = pl.ds(h * count, count)
+        if i == 0:
+            csend[r, 0, 0, rows] = low.astype(bf16)
+            csend[r, 0, 1, rows] = high.astype(bf16)
+            to_col(r, 0, 0, rows)
+            to_col(r, 0, 1, rows)
+        elif i == 1:
+            csend[r, 1, 0, rows] = high.astype(bf16)
+            keep[r, 0, rows] = low
+            to_col(r, 1, 0, rows)
         elif i == 2:
-            csend[r, 1, 1] = low.astype(bf16)
-            keep[r, 1] = high
-            to_col(r, 1, 1)
-        else:
-            keep_own[r, 0] = low
-            keep_own[r, 1] = high
+            csend[r, 1, 1, rows] = low.astype(bf16)
+            keep[r, 1, rows] = high
+            to_col(r, 1, 1, rows)
+        else:
+            keep_own[r, 0, rows] = low
+            keep_own[r, 1, rows] = high
 
     def combine(r, way):
         if r == 0:
@@ -249,9 +260,11 @@
         else:
             gw_sum[:, cols] += part
 
-    arrived(gbuf.at[x, :, other], s_recv)
+    arrived(gbuf.at[x, order[0], other], s_recv.at[0])
+    far_part(other)
+    to_col(0, 0, other)
+    arrived(gbuf.at[x, pl.ds(0, 3), other], s_recv.at[1])
     own_part(other)
-    to_col(0, 0, other)
     to_col(0, 1, core)
 
     steps = dict(
@@ -273,8 +286,8 @@
 def write_results(go, gw, go_out, gw_out, sem):
     copies = []
     for n, (src, dst) in enumerate(((go, go_out), (gw, gw_out))):
-        rows = src.shape[0] // 4
-        for i in range(4):
+        rows = src.shape[0] // 2
+        for i in range(2):
             part = pl.ds(i * rows, rows)
             copies.append(pltpu.make_async_copy(src.at[part], dst.at[part], sem.at[n, i]))
     for copy in copies:
@@ -312,7 +325,7 @@
             pltpu.VMEM((wide, 32 * chunk), bf16),
             pltpu.VMEM((wide, features), f32),
             pltpu.VMEM((wide, features), bf16),
-            dma((3,)), dma((4,)), dma(()), dma((3, 5, 2)), dma((4, 2)), dma((4, 3)), dma((4,)), dma((4, 3)), dma((5,)),
+            dma((3,)), dma((4,)), dma((2,)), dma((3, 5, 2)), dma((4, 2)), dma((4, 3)), dma((4,)), dma((4, 3)), dma((5,)),
         ],
         compiler_params=pltpu.CompilerParams(
             collective_id=0, has_side_effects=True, vmem_limit_bytes=44 * 1024 * 1024
@@ -326,7 +339,7 @@
         ),
         in_specs=[any_spec] * 2,
         out_specs=(any_spec, any_spec),
-        scratch_shapes=[dma((2, 4))],
+        scratch_shapes=[dma((2, 2))],
         compiler_params=pltpu.CompilerParams(vmem_limit_bytes=1024 * 1024),
     )(grad_pre.reshape(tokens, hidden), grad_weight)
 

time: 68.4 us -> 67.8 us (level)
  Pallas kernels: 67.7 us -> 66.4 us
    pallas_call x1, Pallas kernels: 66.1 us -> 64.9 us  [on_device(): pl.pallas_call(kernel, out_shape=(jax.ShapeDtypeStruct((4, chunk, hidden)...]
where the time goes in v5:
time: 67.8 us; the launch traced here: 67.1 us
  Pallas kernels  66.4 us (98%)
    pallas_call x1, Pallas kernels, on_device(): pl.pallas_call(kernel, out_shape=(jax.ShapeDtypeStruct((4, chunk, hidden)...  64.9 us
    pallas_call x1, Pallas kernels, on_device(): pl.pallas_call(write_results, out_shape=(jax.ShapeDtypeStruct((tokens, hi...  1.56 us

profile of v5, /device:TPU:56, one launch (start us, length us, event | category | flops | bytes accessed | tf_op | source)
XLA Modules:
  0.0 67.1 jit_solution(16558507100229611459)
XLA Ops:
  0.6 64.9 %shard_map.50 = (bf16[4,64,3072]{2,1,0:T(8,128)(2,1)S(1)}, bf16[384,1536]{1,0:T(8,128)(2,1)S(1)}) custom-call(bf16[4,2,32,1536]{3,2,1,0:T(8,128)(2,1)} %bitcast.5, bf16[4,64,3072]{2,1,0:T(8,128)(2,1)} %bitcast.4, bf16[384,1536]{1,0:T(8,128)(2,1)} %w_hbm.1), custom_call_target="tpu_custom_call" | custom-call | tf_op jit(solution)/shard_map/pallas_call | solution.py:307
  65.5 1.6 %shard_map.51 = (bf16[256,3072]{1,0:T(8,128)(2,1)}, bf16[384,1536]{1,0:T(8,128)(2,1)}) custom-call(bf16[256,3072]{1,0:T(8,128)(2,1)S(1)} %bitcast.3, bf16[384,1536]{1,0:T(8,128)(2,1)S(1)} %get-tuple-element.5.gw), custom_call_target="tpu_custom_call" | custom-call | tf_op jit(solution)/shard_map/pallas_call | solution.py:334

commit v6 on v5

--- a/solution.py
+++ b/solution.py
@@ -26,16 +26,16 @@
 
 PLAN = [
     ("X", 1, 0), ("X", 3, 0), ("G", 3, 0), ("C", 0, 0), ("C", 0, 1), ("A", 0, 3), ("X", 3, 4), ("G", 1, 0), ("X",
-    1, 4), ("G", 3, 4), ("X", 1, 2), ("G", 1, 4), ("X", 3, 1), ("G", 1, 2), ("G", 3, 1), ("F", 0), ("O", 0), ("P",
-    3, 3), ("X", 1, 1), ("G", 1, 1), ("C", 1, 1), ("A", 0, 1), ("X", 3, 2), ("X", 1, 3), ("P", 3, 1), ("G", 3, 2),
-    ("X", 3, 3), ("C", 1, 0), ("P", 0, 3), ("C", 3, 0), ("C", 3, 1), ("A", 0, 2), ("G", 1, 3), ("A", 0, 0), ("X",
-    2, 4), ("X", 2, 0), ("G", 2, 0), ("G", 2, 4), ("X", 2, 2), ("P", 2, 3), ("W", 0), ("X", 2, 1), ("F", 1), ("G",
-    2, 2), ("P", 3, 2), ("M", 0, 1), ("G", 2, 1), ("G", 3, 3), ("F", 3), ("C", 2, 1), ("P", 1, 3), ("P", 2, 1),
-    ("X", 2, 3), ("C", 2, 0), ("P", 1, 1), ("P", 0, 1), ("G", 2, 3), ("O", 3), ("M", 0, 0), ("F", 2), ("O", 1),
-    ("A", 1, 2), ("A", 1, 0), ("W", 3), ("M", 0, 2), ("A", 3, 3), ("A", 1, 1), ("P", 2, 2), ("A", 3, 1), ("O", 2),
-    ("A", 2, 3), ("P", 0, 2), ("A", 3, 0), ("W", 1), ("A", 1, 3), ("P", 1, 2), ("W", 2), ("R", 3), ("M", 1, 1),
-    ("A", 3, 2), ("A", 2, 2), ("M", 3, 0), ("A", 2, 0), ("M", 1, 2), ("M", 1, 0), ("A", 2, 1), ("M", 2, 0), ("M",
-    3, 2), ("M", 2, 2), ("M", 3, 1), ("M", 2, 1), ("R", 2), ("R", 0), ("R", 1),
+    1, 4), ("G", 3, 4), ("X", 1, 2), ("G", 1, 4), ("X", 3, 1), ("G", 1, 2), ("G", 3, 1), ("P", 3, 3), ("F", 0),
+    ("O", 0), ("X", 1, 1), ("G", 1, 1), ("C", 1, 1), ("A", 0, 1), ("X", 3, 2), ("X", 1, 3), ("P", 3, 1), ("G", 3,
+    2), ("C", 1, 0), ("X", 3, 3), ("P", 0, 3), ("C", 3, 0), ("C", 3, 1), ("A", 0, 2), ("G", 1, 3), ("A", 0, 0),
+    ("X", 2, 4), ("X", 2, 0), ("G", 2, 0), ("G", 2, 4), ("X", 2, 2), ("P", 2, 3), ("W", 0), ("X", 2, 1), ("F", 1),
+    ("G", 2, 2), ("P", 3, 2), ("M", 0, 1), ("G", 2, 1), ("G", 3, 3), ("F", 3), ("C", 2, 1), ("P", 2, 1), ("X", 2,
+    3), ("P", 1, 3), ("P", 1, 1), ("C", 2, 0), ("P", 0, 1), ("G", 2, 3), ("O", 3), ("F", 2), ("O", 1), ("A", 1,
+    2), ("A", 1, 0), ("M", 0, 0), ("W", 3), ("M", 0, 2), ("A", 3, 3), ("A", 1, 1), ("P", 2, 2), ("A", 3, 1), ("O",
+    2), ("A", 2, 3), ("P", 0, 2), ("A", 3, 0), ("A", 3, 2), ("W", 1), ("A", 1, 3), ("P", 1, 2), ("W", 2), ("R",
+    3), ("M", 1, 1), ("A", 2, 2), ("M", 3, 0), ("A", 2, 0), ("M", 1, 2), ("M", 1, 0), ("M", 3, 2), ("A", 2, 1),
+    ("M", 2, 0), ("M", 2, 2), ("M", 3, 1), ("M", 2, 1), ("R", 2), ("R", 0), ("R", 1),
 ]
 
 

time: 67.8 us -> 67.3 us (level)
  no operation moved by 1% of the time
where the time goes in v6:
time: 67.3 us; the launch traced here: 67 us
  Pallas kernels  66.4 us (99%)
    pallas_call x1, Pallas kernels, on_device(): pl.pallas_call(kernel, out_shape=(jax.ShapeDtypeStruct((4, chunk, hidden)...  64.8 us
    pallas_call x1, Pallas kernels, on_device(): pl.pallas_call(write_results, out_shape=(jax.ShapeDtypeStruct((tokens, hi...  1.56 us

profile of v6, /device:TPU:56, one launch (start us, length us, event | category | flops | bytes accessed | tf_op | source)
XLA Modules:
  0.0 67.0 jit_solution(14193923518349632820)
XLA Ops:
  0.6 64.8 %shard_map.50 = (bf16[4,64,3072]{2,1,0:T(8,128)(2,1)S(1)}, bf16[384,1536]{1,0:T(8,128)(2,1)S(1)}) custom-call(bf16[4,2,32,1536]{3,2,1,0:T(8,128)(2,1)} %bitcast.5, bf16[4,64,3072]{2,1,0:T(8,128)(2,1)} %bitcast.4, bf16[384,1536]{1,0:T(8,128)(2,1)} %w_hbm.1), custom_call_target="tpu_custom_call" | custom-call | tf_op jit(solution)/shard_map/pallas_call | solution.py:307
  65.4 1.6 %shard_map.51 = (bf16[256,3072]{1,0:T(8,128)(2,1)}, bf16[384,1536]{1,0:T(8,128)(2,1)}) custom-call(bf16[256,3072]{1,0:T(8,128)(2,1)S(1)} %bitcast.3, bf16[384,1536]{1,0:T(8,128)(2,1)S(1)} %get-tuple-element.5.gw), custom_call_target="tpu_custom_call" | custom-call | tf_op jit(solution)/shard_map/pallas_call | solution.py:334

commit v7 on v6

--- a/solution.py
+++ b/solution.py
@@ -284,12 +284,7 @@
 
 
 def write_results(go, gw, go_out, gw_out, sem):
-    copies = []
-    for n, (src, dst) in enumerate(((go, go_out), (gw, gw_out))):
-        rows = src.shape[0] // 2
-        for i in range(2):
-            part = pl.ds(i * rows, rows)
-            copies.append(pltpu.make_async_copy(src.at[part], dst.at[part], sem.at[n, i]))
+    copies = [pltpu.make_async_copy(go, go_out, sem.at[0]), pltpu.make_async_copy(gw, gw_out, sem.at[1])]
     for copy in copies:
         copy.start()
     for copy in copies:
@@ -339,7 +334,7 @@
         ),
         in_specs=[any_spec] * 2,
         out_specs=(any_spec, any_spec),
-        scratch_shapes=[dma((2, 2))],
+        scratch_shapes=[dma((2,))],
         compiler_params=pltpu.CompilerParams(vmem_limit_bytes=1024 * 1024),
     )(grad_pre.reshape(tokens, hidden), grad_weight)
 

time: 67.3 us -> 67.3 us (level)
  no operation moved by 1% of the time
where the time goes in v7:
time: 67.3 us; the launch traced here: 67 us
  Pallas kernels  66.3 us (99%)
    pallas_call x1, Pallas kernels, on_device(): pl.pallas_call(kernel, out_shape=(jax.ShapeDtypeStruct((4, chunk, hidden)...  64.8 us
    pallas_call x1, Pallas kernels, on_device(): pl.pallas_call(write_results, out_shape=(jax.ShapeDtypeStruct((tokens, hi...  1.55 us

profile of v7, /device:TPU:56, one launch (start us, length us, event | category | flops | bytes accessed | tf_op | source)
XLA Modules:
  0.0 67.0 jit_solution(6032949673845933449)
XLA Ops:
  0.6 64.8 %shard_map.50 = (bf16[4,64,3072]{2,1,0:T(8,128)(2,1)S(1)}, bf16[384,1536]{1,0:T(8,128)(2,1)S(1)}) custom-call(bf16[4,2,32,1536]{3,2,1,0:T(8,128)(2,1)} %bitcast.5, bf16[4,64,3072]{2,1,0:T(8,128)(2,1)} %bitcast.4, bf16[384,1536]{1,0:T(8,128)(2,1)} %w_hbm.1), custom_call_target="tpu_custom_call" | custom-call | tf_op jit(solution)/shard_map/pallas_call | solution.py:302
  65.4 1.6 %shard_map.51 = (bf16[256,3072]{1,0:T(8,128)(2,1)}, bf16[384,1536]{1,0:T(8,128)(2,1)}) custom-call(bf16[256,3072]{1,0:T(8,128)(2,1)S(1)} %bitcast.3, bf16[384,1536]{1,0:T(8,128)(2,1)S(1)} %get-tuple-element.5.gw), custom_call_target="tpu_custom_call" | custom-call | tf_op jit(solution)/shard_map/pallas_call | solution.py:329
